TPU v7x, 256 devices: a whole 4x4x8 slice. The times are simulated.
256 devices in a mesh: expert: 8 (over x, core), replica: 32 (over y, z).
Axes of the slice: x: 4, y: 4, z: 8, core: 2. Of those that a mesh axis runs over, the one named last changes fastest.
Arguments:
- tokens: bfloat16 [1536, 4096], P(('expert', 'replica')), may hold values from -6 to 6
- out_grad: bfloat16 [1536, 4096], P(('expert', 'replica')), may hold values from -2.5 to 2.5
- expert_ids: int32 [1536, 2], P(('expert', 'replica')), may hold values from 0 to 7, all different within a row; in each aligned block of 6 rows (0 to 5, 6 to 11, ...) at most 2 rows name the same one
- gates: float32 [1536, 2], P(('expert', 'replica')), may hold values from 0.1 to 1
- w_gate: bfloat16 [8, 7168, 4096], P('expert', 'replica'), may hold values from -0.09375 to 0.09375
- w_up: bfloat16 [8, 7168, 4096], P('expert', 'replica'), may hold values from -0.09375 to 0.09375
- w_down: bfloat16 [8, 7168, 4096], P('expert', 'replica'), may hold values from -0.0625 to 0.0625
Outputs:
- gate_grad: float32 [1536, 2], P(('expert', 'replica'))
- input_grad: bfloat16 [1536, 4096], P(('expert', 'replica'))
- grad_gate: bfloat16 [8, 7168, 4096], P('expert', 'replica')
- grad_up: bfloat16 [8, 7168, 4096], P('expert', 'replica')
- grad_down: bfloat16 [8, 7168, 4096], P('expert', 'replica')
Inputs may be any that keep to these rules, and one draw needn't show every extreme that they name: `expert_ids`: each row names 2 different experts; among the rows of one device no expert is named more than 2 times.
All inputs are finite; a program needn't handle non-finite values.
Results may differ from a plain program's by a relative error of at most 0.02.
Values may be sent and summed in bfloat16 or wider, within the bound.
No kernel may reach another device: no remote copies, remote signals or barrier semaphores. Data moves between devices by JAX's collectives and lax.ppermute only.
A program may use at most 128 MiB of HBM per device.

v0:
```python
import functools

import jax
import jax.numpy as jnp
from jax import lax
from jax.experimental import pallas as pl
from jax.experimental.pallas import tpu as pltpu
from jax.sharding import Mesh
from jax.sharding import PartitionSpec as P


REPLICA = ("replica_0", "replica_1")
EXPERT_REPLICA = ("expert", "replica_0", "replica_1")
Y = "replica_0"
Z = "replica_1"
LANES = 128
SPLIT = 2560
CHUNK = 512
VMEM = pl.BlockSpec(memory_space=pltpu.VMEM)
SMEM = pl.BlockSpec(memory_space=pltpu.SMEM)
LIMIT = pltpu.CompilerParams(vmem_limit_bytes=16 * 1024 * 1024)
SMALL = pltpu.CompilerParams(vmem_limit_bytes=8 * 1024 * 1024)
CONTRACT = (((1,), (1,)), ((), ()))
LEADING = (((0,), (0,)), ((), ()))


def pass_on(value, axis, back):
    peers = lax.axis_size(axis)
    return lax.ppermute(value, axis, [((i + back) % peers, i) for i in range(peers)])


def direct(value, axis):
    return [value] + [pass_on(value, axis, k) for k in range(1, lax.axis_size(axis))]


def ring(value, axis, split=True):
    middle = lax.axis_size(axis) // 2
    half = value.shape[0] // 2
    ahead = [pass_on(value, axis, 1)]
    behind = [pass_on(value, axis, -1)]
    for _ in range(middle - 2):
        ahead.append(pass_on(ahead[-1], axis, 1))
        behind.append(pass_on(behind[-1], axis, -1))
    if not split:
        return [value] + ahead + [pass_on(ahead[-1], axis, 1)] + behind[::-1]
    first = pass_on(ahead[-1][:half], axis, 1)
    last = pass_on(behind[-1][half:], axis, -1)
    return [value] + ahead + [first, last] + behind[::-1]


def far_first(peers):
    return sorted(range(1, peers), key=lambda k: -min(k, peers - k))


def high_low(value):
    high = value.astype(jnp.bfloat16)
    low = (value - high.astype(jnp.float32)).astype(jnp.bfloat16)
    lane = lax.broadcasted_iota(jnp.int32, (value.shape[0], LANES), 1)
    both = jnp.where(
        lane == 0,
        high.astype(jnp.float32),
        jnp.where(lane == 1, low.astype(jnp.float32), jnp.float32(0)),
    )
    return both.astype(jnp.bfloat16)


def joined(columns):
    return jnp.sum(columns.astype(jnp.float32), axis=1, keepdims=True)


def main_kernel(rows_y, rows_z, slots, count_t, count_s, *refs):
    token_refs, refs = refs[:count_t], refs[count_t:]
    scaled_refs, refs = refs[:count_s], refs[count_s:]
    wg, wu, wd, t_all, s_all, hid_s, gpg_t, upg_t = refs[:8]
    refs = refs[8:]
    out_a, refs = refs[:rows_y], refs[rows_y:]
    out_b, refs = refs[:rows_z], refs[rows_z:]
    acc_g, acc_u, acc_h, val_s, gpg_s, upg_s = refs
    width = t_all.shape[1]
    total = rows_y * rows_z * slots
    acc_g[...] = jnp.zeros_like(acc_g)
    acc_u[...] = jnp.zeros_like(acc_u)
    acc_h[...] = jnp.zeros_like(acc_h)

    def forward(step, carry):
        cols = pl.ds(pl.multiple_of(step * CHUNK, CHUNK), CHUNK)
        for blocks, whole in ((token_refs, t_all), (scaled_refs, s_all)):
            row = 0
            for block in blocks:
                whole[row : row + block.shape[0], cols] = block[:, cols]
                row += block.shape[0]
        rows_t = t_all[:, cols]
        acc_g[...] += lax.dot_general(
            rows_t, wg[:, cols], CONTRACT, preferred_element_type=jnp.float32
        )
        acc_u[...] += lax.dot_general(
            rows_t, wu[:, cols], CONTRACT, preferred_element_type=jnp.float32
        )
        acc_h[...] += lax.dot_general(
            s_all[:, cols], wd[:, cols], CONTRACT, preferred_element_type=jnp.float32
        )
        return carry

    lax.fori_loop(0, width // CHUNK, forward, 0)

    def middle(dz, carry):
        for dy in range(rows_y):
            here = pl.ds(pl.multiple_of((dy * rows_z + dz) * slots, slots), slots)
            there = pl.ds(pl.multiple_of((dz * rows_y + dy) * slots, slots), slots)
            gate_pre = acc_g[here, :]
            up_pre = acc_u[here, :]
            hidden_grad = acc_h[there, :]
            sigmoid_gate = jax.nn.sigmoid(gate_pre)
            active = gate_pre * sigmoid_gate
            hidden = (active * up_pre).astype(jnp.bfloat16)
            val_s[here, :] = high_low(
                jnp.sum(hidden.astype(jnp.float32) * hidden_grad, axis=1, keepdims=True)
            )
            gate_grad = (
                hidden_grad * up_pre * sigmoid_gate * (1.0 + gate_pre * (1.0 - sigmoid_gate))
            ).astype(jnp.bfloat16)
            up_grad = (hidden_grad * active).astype(jnp.bfloat16)
            hid_s[there, :] = hidden
            gpg_t[here, :] = gate_grad
            upg_t[here, :] = up_grad
            gpg_s[there, :] = gate_grad
            upg_s[there, :] = up_grad
        return carry

    lax.fori_loop(0, rows_z, middle, 0, unroll=2)

    def slots_of(left, right, outs, shift):
        rows = total // len(outs)

        def step_of(step, carry):
            cols = pl.ds(pl.multiple_of(step * CHUNK, CHUNK), CHUNK)
            wide = pl.ds(pl.multiple_of(step * CHUNK + shift, CHUNK), CHUNK)
            value = (
                jnp.dot(left[...], wg[:, wide], preferred_element_type=jnp.float32)
                + jnp.dot(right[...], wu[:, wide], preferred_element_type=jnp.float32)
            ).astype(jnp.bfloat16)
            for k, out in enumerate(outs):
                out[:, cols] = value[k * rows : (k + 1) * rows]
            return carry

        return step_of

    lax.fori_loop(0, SPLIT // CHUNK, slots_of(gpg_t, upg_t, out_a, 0), 0)
    for k, out in enumerate(out_a):
        rows = total // rows_y
        out[:, SPLIT:] = val_s[k * rows : (k + 1) * rows, :]
    lax.fori_loop(0, (width - SPLIT) // CHUNK, slots_of(gpg_s, upg_s, out_b, SPLIT), 0)


def main_call(token_blocks, scaled_blocks, wg, wu, wd, rows_y, rows_z, slots):
    total = rows_y * rows_z * slots
    hidden, width = wg.shape
    bf = jnp.bfloat16
    shapes = [jax.ShapeDtypeStruct((total, width), bf)] * 2
    shapes += [jax.ShapeDtypeStruct((total, hidden), bf)] * 3
    shapes += [jax.ShapeDtypeStruct((total // rows_y, SPLIT + LANES), bf)] * rows_y
    shapes += [jax.ShapeDtypeStruct((total // rows_z, width - SPLIT), bf)] * rows_z
    blocks = list(token_blocks) + list(scaled_blocks)
    outs = pl.pallas_call(
        functools.partial(
            main_kernel, rows_y, rows_z, slots, len(token_blocks), len(scaled_blocks)
        ),
        out_shape=shapes,
        in_specs=[VMEM] * (len(blocks) + 3),
        out_specs=[VMEM] * len(shapes),
        scratch_shapes=[pltpu.VMEM((total, hidden), jnp.float32)] * 3
        + [pltpu.VMEM((total, LANES), bf)]
        + [pltpu.VMEM((total, hidden), bf)] * 2,
        compiler_params=LIMIT,
        cost_estimate=pl.CostEstimate(
            flops=10 * total * hidden * width, bytes_accessed=30 << 20, transcendentals=0
        ),
        name="experts",
    )(*blocks, wg, wu, wd)
    return outs[:5], outs[5 : 5 + rows_y], outs[5 + rows_y :]


def add_narrow(ins, rows, out):
    value = joined(ins[0][rows, SPLIT:])
    for ref in ins[1:]:
        value = value + joined(ref[rows, SPLIT:])
    out[:, SPLIT:] = high_low(value)


def sum_a_kernel(slots, *refs):
    outs = refs[-(refs[0].shape[0] // slots) :]
    ins = refs[: len(refs) - len(outs)]

    def step(index, carry):
        cols = pl.ds(pl.multiple_of(index * LANES, LANES), LANES)
        for k, out in enumerate(outs):
            rows = slice(k * slots, (k + 1) * slots)
            total = ins[0][rows, cols].astype(jnp.float32)
            for ref in ins[1:]:
                total = total + ref[rows, cols].astype(jnp.float32)
            out[:, cols] = total.astype(jnp.bfloat16)
        return carry

    lax.fori_loop(0, SPLIT // LANES, step, 0)
    for k, out in enumerate(outs):
        add_narrow(ins, slice(k * slots, (k + 1) * slots), out)


def sum_b_kernel(slots, place, *refs):
    ins, out = refs[:-1], refs[-1]
    peers, owners, capacity = out.shape[0], out.shape[1], out.shape[2]

    def step(k, carry):
        rows = pl.ds(pl.multiple_of(k * slots, slots), slots)
        target = lax.rem(place[0] + k, peers)
        total = ins[0][rows, :].astype(jnp.float32)
        for ref in ins[1:]:
            total = total + ref[rows, :].astype(jnp.float32)
        total = total.astype(jnp.bfloat16)
        for e in range(owners):
            out[target, e] = total[e * capacity : (e + 1) * capacity]
        return carry

    lax.fori_loop(0, peers, step, 0)


def last_kernel(*refs):
    ins, out = refs[:-1], refs[-1]

    def step(index, carry):
        cols = pl.ds(pl.multiple_of(index * CHUNK, CHUNK), CHUNK)
        total = ins[0][:, cols].astype(jnp.float32)
        for ref in ins[1:]:
            total = total + ref[:, cols].astype(jnp.float32)
        out[:, cols] = total.astype(jnp.bfloat16)
        return carry

    lax.fori_loop(0, SPLIT // CHUNK, step, 0)
    add_narrow(ins, slice(None), out)


def cost(count):
    return pl.CostEstimate(flops=count, bytes_accessed=3 * count, transcendentals=0)


def on_device(tokens, out_grad, expert_ids, gates, w_gate, w_up, w_down):
    token_count = tokens.shape[0]
    fan_out = expert_ids.shape[1]
    model_width = tokens.shape[1]
    owners = lax.axis_size("expert")
    rows_y = lax.axis_size(Y)
    rows_z = lax.axis_size(Z)
    capacity = max(2, 4 * token_count * fan_out // (3 * owners))
    slots = owners * capacity
    bf = jnp.bfloat16
    flat_ids = expert_ids.reshape(-1)
    sequence_pos = jnp.arange(token_count * fan_out, dtype=jnp.int32)
    earlier = sequence_pos[None, :] < sequence_pos[:, None]
    same_expert = flat_ids[:, None] == flat_ids[None, :]
    slot_rank = jnp.sum(jnp.logical_and(same_expert, earlier), axis=1)
    target = flat_ids * capacity + slot_rank
    token_hot = (target[:, None] == jnp.arange(slots, dtype=jnp.int32)[None, :]).astype(jnp.float32)
    token_hot = token_hot.reshape(token_count, fan_out, slots)
    dispatch = jnp.sum(token_hot, axis=1).astype(bf)
    slot_gate = jnp.sum(token_hot * gates[:, :, None], axis=(0, 1))
    picked = lax.dot_general(
        dispatch,
        jnp.concatenate([tokens, out_grad], axis=1),
        LEADING,
        preferred_element_type=jnp.float32,
    )
    scale = jnp.concatenate(
        [
            jnp.ones((slots, model_width), jnp.float32),
            jnp.broadcast_to(slot_gate[:, None], (slots, model_width)),
        ],
        axis=1,
    )
    send = (picked * scale).astype(bf)
    owned = lax.all_to_all(
        send.reshape(owners, capacity, 2 * model_width), "expert", 0, 0, tiled=True
    ).reshape(slots, 2 * model_width)
    owned, place = lax.optimization_barrier((owned, lax.axis_index(Y).reshape(1)))
    scaled_y = jnp.concatenate(direct(owned[:, model_width:], Y), axis=0)
    tokens_z = jnp.concatenate(
        ring(owned[:, :model_width], Z, split=False), axis=0
    )
    token_blocks = ring(tokens_z, Y)
    scaled_blocks = ring(scaled_y, Z)
    (gathered, scaled, hidden, gate_pre_grad, up_pre_grad), out_a, out_b = main_call(
        token_blocks, scaled_blocks, w_gate[0], w_up[0], w_down[0], rows_y, rows_z, slots
    )
    arrived_b = [pass_on(out_b[k], Z, -k) for k in far_first(rows_z)]
    arrived_a = [pass_on(out_a[k], Y, -k) for k in range(1, rows_y)]
    grad_down = lax.dot_general(
        hidden, scaled, LEADING, preferred_element_type=jnp.float32
    ).astype(bf)
    grad_gate = lax.dot_general(
        gate_pre_grad, gathered, LEADING, preferred_element_type=jnp.float32
    ).astype(bf)
    grad_up = lax.dot_general(
        up_pre_grad, gathered, LEADING, preferred_element_type=jnp.float32
    ).astype(bf)
    wide = SPLIT + LANES
    narrow = model_width - SPLIT
    tiles_b = pl.pallas_call(
        functools.partial(sum_b_kernel, slots),
        out_shape=jax.ShapeDtypeStruct((rows_y, owners, capacity, narrow), bf),
        in_specs=[SMEM] + [VMEM] * rows_z,
        out_specs=VMEM,
        compiler_params=SMALL,
        cost_estimate=cost(rows_y * rows_z * slots * narrow),
        name="sum_z",
    )(place, out_b[0], *arrived_b)
    back_b = lax.all_to_all(
        tiles_b.reshape(rows_y * owners, capacity, narrow), (Y, "expert"), 0, 0, tiled=True
    ).reshape(rows_y * slots, narrow)
    tiles_a = pl.pallas_call(
        functools.partial(sum_a_kernel, slots),
        out_shape=[jax.ShapeDtypeStruct((slots, wide), bf)] * rows_z,
        in_specs=[VMEM] * rows_y,
        out_specs=[VMEM] * rows_z,
        compiler_params=SMALL,
        cost_estimate=cost(rows_y * rows_z * slots * wide),
        name="sum_y",
    )(out_a[0], *arrived_a)
    moved_a = [pass_on(tiles_a[k], Z, -k) for k in far_first(rows_z)]
    slot_home = pl.pallas_call(
        last_kernel,
        out_shape=jax.ShapeDtypeStruct((slots, wide), bf),
        in_specs=[VMEM] * rows_z,
        out_specs=VMEM,
        compiler_params=SMALL,
        cost_estimate=cost(rows_z * slots * wide),
        name="sum_home",
    )(tiles_a[0], *moved_a)
    back_a = lax.all_to_all(
        slot_home.reshape(owners, capacity, wide), "expert", 0, 0, tiled=True
    ).reshape(slots, wide)

    def combine(times, value):
        return jnp.dot(
            jnp.concatenate([dispatch] * times, axis=1), value, preferred_element_type=jnp.float32
        )

    input_grad = jnp.concatenate(
        [combine(1, back_a[:, :SPLIT]), combine(rows_y, back_b)], axis=1
    ).astype(bf)
    returned = joined(back_a[:, SPLIT:])
    product = jnp.sum(token_hot * returned[None, None, :, 0], axis=2)
    gate_grad = product / gates
    return (gate_grad, input_grad, grad_gate[None], grad_up[None], grad_down[None])


def solution(mesh):
    torus = Mesh(
        mesh.devices.reshape(mesh.shape["expert"], 4, 8), ("expert", "replica_0", "replica_1")
    )
    in_specs = (
        P(EXPERT_REPLICA, None),
        P(EXPERT_REPLICA, None),
        P(EXPERT_REPLICA, None),
        P(EXPERT_REPLICA, None),
        P("expert", REPLICA, None),
        P("expert", REPLICA, None),
        P("expert", REPLICA, None),
    )
    out_specs = (
        P(EXPERT_REPLICA, None),
        P(EXPERT_REPLICA, None),
        P("expert", REPLICA, None),
        P("expert", REPLICA, None),
        P("expert", REPLICA, None),
    )

    return jax.shard_map(
        on_device, mesh=torus, in_specs=in_specs, out_specs=out_specs, check_vma=False
    )
```

profile of v0, /device:TPU:1, one launch (start us, length us, event | category | flops | bytes accessed | tf_op | source)
XLA Modules:
  0.0 190.6 jit_solution(9204447867656367987)
XLA Ops:
  4.8 6.5 %all-to-all-start = ((bf16[8,2,8192]{2,1,0:T(2,128)(2,1)}), bf16[8,2,8192]{2,1,0:T(2,128)(2,1)S(1)}, u32[]{:S(2)}, u32[]{:S(2)}) async-start(bf16[8,2,8192]{2,1,0:T(2,128)(2,1)} %reshape.54), calls=%async_computation | async-start | bytes 524288 | tf_op jit(solution)/shard_map/all_to_all | solution.py:280
  11.3 6.5 %all-to-all-done = bf16[8,2,8192]{2,1,0:T(2,128)(2,1)S(1)} async-done(((bf16[8,2,8192]{2,1,0:T(2,128)(2,1)}), bf16[8,2,8192]{2,1,0:T(2,128)(2,1)S(1)}, u32[]{:S(2)}, u32[]{:S(2)}) %all-to-all-start) | async-done | bytes 262176 | tf_op jit(solution)/shard_map/all_to_all | solution.py:280
  23.9 3.9 %collective-permute-start = (bf16[16,4096]{1,0:T(8,128)(2,1)S(1)}, bf16[16,4096]{1,0:T(8,128)(2,1)S(1)}, u32[]{:S(2)}, u32[]{:S(2)}) collective-permute-start(bf16[16,4096]{1,0:T(8,128)(2,1)S(1)} %get-tuple-element.68), channel_id=1, source_target_pairs={{1,0},{2,1},{3,2},{4,3},{5,4},{6,5},{7,6},{0,7},{9,8},{10,9},{11,1... | collective-permute-start | bytes 393224 | tf_op jit(solution)/shard_map/ppermute | solution.py:29
  28.4 4.0 %collective-permute-start.14 = (bf16[64,4096]{1,0:T(8,128)(2,1)S(1)}, bf16[64,4096]{1,0:T(8,128)(2,1)S(1)}, u32[]{:S(2)}, u32[]{:S(2)}) collective-permute-start(bf16[64,4096]{1,0:T(8,128)(2,1)S(1)} %pad_maximum_fusion.refs_5_), channel_id=1, source_target_pairs={{1,0},{2,1},{3,2},{4,3},{5,4},{6,5},{7,6},{0,7},{9,8},{10,9},{11,1... | collective-permute-start | bytes 1572872 | tf_op jit(solution)/shard_map/ppermute | solution.py:29
  35.2 10.6 %collective-permute-done.5 = bf16[16,4096]{1,0:T(8,128)(2,1)S(1)} collective-permute-done((bf16[16,4096]{1,0:T(8,128)(2,1)S(1)}, bf16[16,4096]{1,0:T(8,128)(2,1)S(1)}, u32[]{:S(2)}, u32[]{:S(2)}) %collective-permute-start.5) | collective-permute-done | bytes 131104 | tf_op jit(solution)/shard_map/ppermute | solution.py:29
  50.4 3.1 %collective-permute-start.3 = (bf16[16,4096]{1,0:T(8,128)(2,1)S(1)}, bf16[16,4096]{1,0:T(8,128)(2,1)S(1)}, u32[]{:S(2)}, u32[]{:S(2)}) collective-permute-start(bf16[16,4096]{1,0:T(8,128)(2,1)S(1)} %collective-permute-done.2), channel_id=1, source_target_pairs={{1,0},{2,1},{3,2},{4,3},{5,4},{6,5},{7,6},{0,7},{9,8},{10,9},{11,1... | collective-permute-start | bytes 393224 | tf_op jit(solution)/shard_map/ppermute | solution.py:29
  58.5 3.3 %collective-permute-start.15 = (bf16[64,4096]{1,0:T(8,128)(2,1)S(1)}, bf16[64,4096]{1,0:T(8,128)(2,1)S(1)}, u32[]{:S(2)}, u32[]{:S(2)}) collective-permute-start(bf16[64,4096]{1,0:T(8,128)(2,1)S(1)} %collective-permute-done.14.refs_6_), channel_id=1, source_target_pairs={{1,0},{2,1},{3,2},{4,3},{5,4},{6,5},{7,6},{0,7},{9,8},{10,9},{11,1... | collective-permute-start | bytes 1572872 | tf_op jit(solution)/shard_map/ppermute | solution.py:29
  61.9 6.8 %collective-permute-done.19.refs_12_ = bf16[64,4096]{1,0:T(8,128)(2,1)S(1)} collective-permute-done((bf16[64,4096]{1,0:T(8,128)(2,1)S(1)}, bf16[64,4096]{1,0:T(8,128)(2,1)S(1)}, u32[]{:S(2)}, u32[]{:S(2)}) %collective-permute-start.19) | collective-permute-done | bytes 524320 | tf_op jit(solution)/shard_map/ppermute | solution.py:29
  71.4 5.9 %collective-permute-done.9.refs_4_ = bf16[128,4096]{1,0:T(8,128)(2,1)S(1)} collective-permute-done((bf16[128,4096]{1,0:T(8,128)(2,1)S(1)}, bf16[128,4096]{1,0:T(8,128)(2,1)S(1)}, u32[]{:S(2)}, u32[]{:S(2)}) %collective-permute-start.9) | collective-permute-done | bytes 1048608 | tf_op jit(solution)/shard_map/ppermute | solution.py:29
  77.4 2.7 %collective-permute-start.8 = (bf16[64,4096]{1,0:T(8,128)(2,1)S(1)}, bf16[64,4096]{1,0:T(8,128)(2,1)S(1)}, u32[]{:S(2)}, u32[]{:S(2)}) collective-permute-start(bf16[64,4096]{1,0:T(8,128)(2,1)S(1)} %slice.32), channel_id=1, source_target_pairs={{8,0},{16,8},{24,16},{0,24},{9,1},{17,9},{25,17},{1,25},{10,2},{18... | collective-permute-start | bytes 1572872 | tf_op jit(solution)/shard_map/ppermute | solution.py:29
  80.3 2.9 %collective-permute-start.17 = (bf16[32,4096]{1,0:T(8,128)(2,1)S(1)}, bf16[32,4096]{1,0:T(8,128)(2,1)S(1)}, u32[]{:S(2)}, u32[]{:S(2)}) collective-permute-start(bf16[32,4096]{1,0:T(8,128)(2,1)S(1)} %slice.34), channel_id=1, source_target_pairs={{1,0},{2,1},{3,2},{4,3},{5,4},{6,5},{7,6},{0,7},{9,8},{10,9},{11,1... | collective-permute-start | bytes 786440 | tf_op jit(solution)/shard_map/ppermute | solution.py:29
  83.2 5.6 %collective-permute-done.21.refs_10_ = bf16[32,4096]{1,0:T(8,128)(2,1)S(1)} collective-permute-done((bf16[32,4096]{1,0:T(8,128)(2,1)S(1)}, bf16[32,4096]{1,0:T(8,128)(2,1)S(1)}, u32[]{:S(2)}, u32[]{:S(2)}) %collective-permute-start.21) | collective-permute-done | bytes 262176 | tf_op jit(solution)/shard_map/ppermute | solution.py:29
  89.3 9.2 %experts.1 = (bf16[512,4096]{1,0:T(8,128)(2,1)S(1)}, bf16[512,4096]{1,0:T(8,128)(2,1)S(1)}, bf16[512,224]{1,0:T(8,128)(2,1)S(1)}, bf16[512,224]{1,0:T(8,128)(2,1...) custom-call(bf16[128,4096]{1,0:T(8,128)(2,1)S(1)} %constant_dynamic-, ...), custom_call_target="tpu_custom_call" | custom-call | flops 4697620480 | bytes 31457280 | tf_op jit(solution)/shard_map/experts/pallas_call | solution.py:164
  101.7 3.7 %collective-permute-start.32 = (bf16[64,1536]{1,0:T(8,128)(2,1)S(1)}, bf16[64,1536]{1,0:T(8,128)(2,1)S(1)}, u32[]{:S(2)}, u32[]{:S(2)}) collective-permute-start(bf16[64,1536]{1,0:T(8,128)(2,1)S(1)} %get-tuple-element.47), channel_id=1, source_target_pairs={{4,0},{5,1},{6,2},{7,3},{0,4},{1,5},{2,6},{3,7},{12,8},{13,9},{14,... | collective-permute-start | bytes 589832 | tf_op jit(solution)/shard_map/ppermute | solution.py:29
  107.8 4.2 %collective-permute-done.22.refs_1_ = bf16[128,2688]{1,0:T(8,128)(2,1)S(1)} collective-permute-done((bf16[128,2688]{1,0:T(8,128)(2,1)S(1)}, bf16[128,2688]{1,0:T(8,128)(2,1)S(1)}, u32[]{:S(2)}, u32[]{:S(2)}) %collective-permute-start.22) | collective-permute-done | bytes 688160 | tf_op jit(solution)/shard_map/ppermute | solution.py:29
  113.5 9.3 %collective-permute-done.23.refs_2_ = bf16[128,2688]{1,0:T(8,128)(2,1)S(1)} collective-permute-done((bf16[128,2688]{1,0:T(8,128)(2,1)S(1)}, bf16[128,2688]{1,0:T(8,128)(2,1)S(1)}, u32[]{:S(2)}, u32[]{:S(2)}) %collective-permute-start.23) | collective-permute-done | bytes 688160 | tf_op jit(solution)/shard_map/ppermute | solution.py:29
  122.8 3.3 %collective-permute-start.35 = (bf16[64,1536]{1,0:T(8,128)(2,1)S(1)}, bf16[64,1536]{1,0:T(8,128)(2,1)S(1)}, u32[]{:S(2)}, u32[]{:S(2)}) collective-permute-start(bf16[64,1536]{1,0:T(8,128)(2,1)S(1)} %get-tuple-element.50), channel_id=1, source_target_pairs={{6,0},{7,1},{0,2},{1,3},{2,4},{3,5},{4,6},{5,7},{14,8},{15,9},{8,1... | collective-permute-start | bytes 589832 | tf_op jit(solution)/shard_map/ppermute | solution.py:29
  130.6 3.3 %collective-permute-start.36 = (bf16[64,1536]{1,0:T(8,128)(2,1)S(1)}, bf16[64,1536]{1,0:T(8,128)(2,1)S(1)}, u32[]{:S(2)}, u32[]{:S(2)}) collective-permute-start(bf16[64,1536]{1,0:T(8,128)(2,1)S(1)} %get-tuple-element.51), channel_id=1, source_target_pairs={{2,0},{3,1},{4,2},{5,3},{6,4},{7,5},{0,6},{1,7},{10,8},{11,9},{12,... | collective-permute-start | bytes 589832 | tf_op jit(solution)/shard_map/ppermute | solution.py:29
  137.2 3.4 %collective-permute-start.25 = (bf16[16,2688]{1,0:T(8,128)(2,1)S(1)}, bf16[16,2688]{1,0:T(8,128)(2,1)S(1)}, u32[]{:S(2)}, u32[]{:S(2)}) collective-permute-start(bf16[16,2688]{1,0:T(8,128)(2,1)S(1)} %get-tuple-element.38), channel_id=1, source_target_pairs={{4,0},{5,1},{6,2},{7,3},{0,4},{1,5},{2,6},{3,7},{12,8},{13,9},{14,... | collective-permute-start | bytes 258056 | tf_op jit(solution)/shard_map/ppermute | solution.py:29
  143.0 6.6 %collective-permute-done.38.refs_7_ = bf16[64,1536]{1,0:T(8,128)(2,1)S(1)} collective-permute-done((bf16[64,1536]{1,0:T(8,128)(2,1)S(1)}, bf16[64,1536]{1,0:T(8,128)(2,1)S(1)}, u32[]{:S(2)}, u32[]{:S(2)}) %collective-permute-start.38) | collective-permute-done | bytes 196640 | tf_op jit(solution)/shard_map/ppermute | solution.py:29
  150.5 12.3 %all-to-all-start.2 = ((bf16[32,2,1536]{2,1,0:T(2,128)(2,1)}), bf16[32,2,1536]{2,1,0:T(2,128)(2,1)S(1)}, u32[]{:S(2)}, u32[]{:S(2)}) async-start(bf16[32,2,1536]{2,1,0:T(2,128)(2,1)} %bitcast.4), calls=%async_computation.2 | async-start | bytes 393216 | tf_op jit(solution)/shard_map/all_to_all | solution.py:315
  171.3 4.6 %fusion.3 = bf16[1,224,4096]{2,1,0:T(8,128)(2,1)} fusion(bf16[512,224]{1,0:T(8,128)(2,1)S(1)} %get-tuple-element.57, bf16[512,4096]{1,0:T(8,128)(2,1)} %copy-done), kind=kOutput, calls=%fused_computation.7 | convolution fusion | flops 940441600 | bytes 6258688 | tf_op jit(solution)/shard_map/dot_general | solution.py:295
  178.7 5.2 %all-to-all-start.1 = ((bf16[8,2,2688]{2,1,0:T(2,128)(2,1)}), bf16[8,2,2688]{2,1,0:T(2,128)(2,1)S(1)}, u32[]{:S(2)}, u32[]{:S(2)}) async-start(bf16[8,2,2688]{2,1,0:T(2,128)(2,1)} %reshape.57), calls=%async_computation.1 | async-start | bytes 172032 | tf_op jit(solution)/shard_map/all_to_all | solution.py:337
  184.2 4.7 %all-to-all-done.1 = bf16[8,2,2688]{2,1,0:T(2,128)(2,1)S(1)} async-done(((bf16[8,2,2688]{2,1,0:T(2,128)(2,1)}), bf16[8,2,2688]{2,1,0:T(2,128)(2,1)S(1)}, u32[]{:S(2)}, u32[]{:S(2)}) %all-to-all-start.1) | async-done | bytes 86048 | tf_op jit(solution)/shard_map/all_to_all | solution.py:337
  (109 shorter events, 58.1 us)
Async XLA Ops:
  4.8 13.0 %all-to-all-start = ((bf16[8,2,8192]{2,1,0:T(2,128)(2,1)}), bf16[8,2,8192]{2,1,0:T(2,128)(2,1)S(1)}, u32[]{:S(2)}, u32[]{:S(2)}) async-start(bf16[8,2,8192]{2,1,0:T(2,128)(2,1)} %reshape.54), calls=%async_computation | async-start | bytes 524288 | tf_op jit(solution)/shard_map/all_to_all | solution.py:280
  27.9 30.6 %collective-permute-start.18 = (bf16[64,4096]{1,0:T(8,128)(2,1)S(1)}, bf16[64,4096]{1,0:T(8,128)(2,1)S(1)}, u32[]{:S(2)}, u32[]{:S(2)}) collective-permute-start(bf16[64,4096]{1,0:T(8,128)(2,1)S(1)} %pad_maximum_fusion.refs_5_), channel_id=1, source_target_pairs={{7,0},{0,1},{1,2},{2,3},{3,4},{4,5},{5,6},{6,7},{15,8},{8,9},{9,10... | collective-permute-start | bytes 1572872 | tf_op jit(solution)/shard_map/ppermute | solution.py:29
  28.4 30.1 %collective-permute-start.14 = (bf16[64,4096]{1,0:T(8,128)(2,1)S(1)}, bf16[64,4096]{1,0:T(8,128)(2,1)S(1)}, u32[]{:S(2)}, u32[]{:S(2)}) collective-permute-start(bf16[64,4096]{1,0:T(8,128)(2,1)S(1)} %pad_maximum_fusion.refs_5_), channel_id=1, source_target_pairs={{1,0},{2,1},{3,2},{4,3},{5,4},{6,5},{7,6},{0,7},{9,8},{10,9},{11,1... | collective-permute-start | bytes 1572872 | tf_op jit(solution)/shard_map/ppermute | solution.py:29
  32.5 13.3 %collective-permute-start.5 = (bf16[16,4096]{1,0:T(8,128)(2,1)S(1)}, bf16[16,4096]{1,0:T(8,128)(2,1)S(1)}, u32[]{:S(2)}, u32[]{:S(2)}) collective-permute-start(bf16[16,4096]{1,0:T(8,128)(2,1)S(1)} %collective-permute-done.4), channel_id=1, source_target_pairs={{7,0},{0,1},{1,2},{2,3},{3,4},{4,5},{5,6},{6,7},{15,8},{8,9},{9,10... | collective-permute-start | bytes 393224 | tf_op jit(solution)/shard_map/ppermute | solution.py:29
  32.5 13.3 %collective-permute-start.1 = (bf16[16,4096]{1,0:T(8,128)(2,1)S(1)}, bf16[16,4096]{1,0:T(8,128)(2,1)S(1)}, u32[]{:S(2)}, u32[]{:S(2)}) collective-permute-start(bf16[16,4096]{1,0:T(8,128)(2,1)S(1)} %collective-permute-done), channel_id=1, source_target_pairs={{1,0},{2,1},{3,2},{4,3},{5,4},{6,5},{7,6},{0,7},{9,8},{10,9},{11,1... | collective-permute-start | bytes 393224 | tf_op jit(solution)/shard_map/ppermute | solution.py:29
  55.5 21.8 %collective-permute-start.9 = (bf16[128,4096]{1,0:T(8,128)(2,1)S(1)}, bf16[128,4096]{1,0:T(8,128)(2,1)S(1)}, u32[]{:S(2)}, u32[]{:S(2)}) collective-permute-start(bf16[128,4096]{1,0:T(8,128)(2,1)S(1)} %constant_dynamic-update-slice_fusion.refs_0_), channel_id=1, source_target_pairs={{24,0},{0,8},{8,16},{16,24},{25,1},{1,9},{9,17},{17,25},{26,2},{2,... | collective-permute-start | bytes 3145736 | tf_op jit(solution)/shard_map/ppermute | solution.py:29
  56.8 20.6 %collective-permute-start.7 = (bf16[128,4096]{1,0:T(8,128)(2,1)S(1)}, bf16[128,4096]{1,0:T(8,128)(2,1)S(1)}, u32[]{:S(2)}, u32[]{:S(2)}) collective-permute-start(bf16[128,4096]{1,0:T(8,128)(2,1)S(1)} %constant_dynamic-update-slice_fusion.refs_0_), channel_id=1, source_target_pairs={{8,0},{16,8},{24,16},{0,24},{9,1},{17,9},{25,17},{1,25},{10,2},{18... | collective-permute-start | bytes 3145736 | tf_op jit(solution)/shard_map/ppermute | solution.py:29
  68.7 11.5 %collective-permute-start.20 = (bf16[64,4096]{1,0:T(8,128)(2,1)S(1)}, bf16[64,4096]{1,0:T(8,128)(2,1)S(1)}, u32[]{:S(2)}, u32[]{:S(2)}) collective-permute-start(bf16[64,4096]{1,0:T(8,128)(2,1)S(1)} %collective-permute-done.19.refs_12_), channel_id=1, source_target_pairs={{7,0},{0,1},{1,2},{2,3},{3,4},{4,5},{5,6},{6,7},{15,8},{8,9},{9,10... | collective-permute-start | bytes 1572872 | tf_op jit(solution)/shard_map/ppermute | solution.py:29
  68.7 11.6 %collective-permute-start.16 = (bf16[64,4096]{1,0:T(8,128)(2,1)S(1)}, bf16[64,4096]{1,0:T(8,128)(2,1)S(1)}, u32[]{:S(2)}, u32[]{:S(2)}) collective-permute-start(bf16[64,4096]{1,0:T(8,128)(2,1)S(1)} %collective-permute-done.15.refs_7_), channel_id=1, source_target_pairs={{1,0},{2,1},{3,2},{4,3},{5,4},{6,5},{7,6},{0,7},{9,8},{10,9},{11,1... | collective-permute-start | bytes 1572872 | tf_op jit(solution)/shard_map/ppermute | solution.py:29
  77.3 12.0 %collective-permute-start.10 = (bf16[64,4096]{1,0:T(8,128)(2,1)S(1)}, bf16[64,4096]{1,0:T(8,128)(2,1)S(1)}, u32[]{:S(2)}, u32[]{:S(2)}) collective-permute-start(bf16[64,4096]{1,0:T(8,128)(2,1)S(1)} %slice.33), channel_id=1, source_target_pairs={{24,0},{0,8},{8,16},{16,24},{25,1},{1,9},{9,17},{17,25},{26,2},{2,... | collective-permute-start | bytes 1572872 | tf_op jit(solution)/shard_map/ppermute | solution.py:29
  77.4 11.8 %collective-permute-start.8 = (bf16[64,4096]{1,0:T(8,128)(2,1)S(1)}, bf16[64,4096]{1,0:T(8,128)(2,1)S(1)}, u32[]{:S(2)}, u32[]{:S(2)}) collective-permute-start(bf16[64,4096]{1,0:T(8,128)(2,1)S(1)} %slice.32), channel_id=1, source_target_pairs={{8,0},{16,8},{24,16},{0,24},{9,1},{17,9},{25,17},{1,25},{10,2},{18... | collective-permute-start | bytes 1572872 | tf_op jit(solution)/shard_map/ppermute | solution.py:29
  98.5 13.5 %collective-permute-start.22 = (bf16[128,2688]{1,0:T(8,128)(2,1)S(1)}, bf16[128,2688]{1,0:T(8,128)(2,1)S(1)}, u32[]{:S(2)}, u32[]{:S(2)}) collective-permute-start(bf16[128,2688]{1,0:T(8,128)(2,1)S(1)} %get-tuple-element.34), channel_id=1, source_target_pairs={{24,0},{0,8},{8,16},{16,24},{25,1},{1,9},{9,17},{17,25},{26,2},{2,... | collective-permute-start | bytes 2064392 | tf_op jit(solution)/shard_map/ppermute | solution.py:29
  98.5 24.3 %collective-permute-start.23 = (bf16[128,2688]{1,0:T(8,128)(2,1)S(1)}, bf16[128,2688]{1,0:T(8,128)(2,1)S(1)}, u32[]{:S(2)}, u32[]{:S(2)}) collective-permute-start(bf16[128,2688]{1,0:T(8,128)(2,1)S(1)} %get-tuple-element.35), channel_id=1, source_target_pairs={{16,0},{24,8},{0,16},{8,24},{17,1},{25,9},{1,17},{9,25},{18,2},{26... | collective-permute-start | bytes 2064392 | tf_op jit(solution)/shard_map/ppermute | solution.py:29
  100.7 29.9 %collective-permute-start.24 = (bf16[128,2688]{1,0:T(8,128)(2,1)S(1)}, bf16[128,2688]{1,0:T(8,128)(2,1)S(1)}, u32[]{:S(2)}, u32[]{:S(2)}) collective-permute-start(bf16[128,2688]{1,0:T(8,128)(2,1)S(1)} %get-tuple-element.36), channel_id=1, source_target_pairs={{8,0},{16,8},{24,16},{0,24},{9,1},{17,9},{25,17},{1,25},{10,2},{18... | collective-permute-start | bytes 2064392 | tf_op jit(solution)/shard_map/ppermute | solution.py:29
  101.7 32.7 %collective-permute-start.32 = (bf16[64,1536]{1,0:T(8,128)(2,1)S(1)}, bf16[64,1536]{1,0:T(8,128)(2,1)S(1)}, u32[]{:S(2)}, u32[]{:S(2)}) collective-permute-start(bf16[64,1536]{1,0:T(8,128)(2,1)S(1)} %get-tuple-element.47), channel_id=1, source_target_pairs={{4,0},{5,1},{6,2},{7,3},{0,4},{1,5},{2,6},{3,7},{12,8},{13,9},{14,... | collective-permute-start | bytes 589832 | tf_op jit(solution)/shard_map/ppermute | solution.py:29
  105.5 29.7 %collective-permute-start.33 = (bf16[64,1536]{1,0:T(8,128)(2,1)S(1)}, bf16[64,1536]{1,0:T(8,128)(2,1)S(1)}, u32[]{:S(2)}, u32[]{:S(2)}) collective-permute-start(bf16[64,1536]{1,0:T(8,128)(2,1)S(1)} %get-tuple-element.48), channel_id=1, source_target_pairs={{5,0},{6,1},{7,2},{0,3},{1,4},{2,5},{3,6},{4,7},{13,8},{14,9},{15,... | collective-permute-start | bytes 589832 | tf_op jit(solution)/shard_map/ppermute | solution.py:29
  112.0 25.2 %collective-permute-start.34 = (bf16[64,1536]{1,0:T(8,128)(2,1)S(1)}, bf16[64,1536]{1,0:T(8,128)(2,1)S(1)}, u32[]{:S(2)}, u32[]{:S(2)}) collective-permute-start(bf16[64,1536]{1,0:T(8,128)(2,1)S(1)} %get-tuple-element.49), channel_id=1, source_target_pairs={{3,0},{4,1},{5,2},{6,3},{7,4},{0,5},{1,6},{2,7},{11,8},{12,9},{13,... | collective-permute-start | bytes 589832 | tf_op jit(solution)/shard_map/ppermute | solution.py:29
  122.8 17.8 %collective-permute-start.35 = (bf16[64,1536]{1,0:T(8,128)(2,1)S(1)}, bf16[64,1536]{1,0:T(8,128)(2,1)S(1)}, u32[]{:S(2)}, u32[]{:S(2)}) collective-permute-start(bf16[64,1536]{1,0:T(8,128)(2,1)S(1)} %get-tuple-element.50), channel_id=1, source_target_pairs={{6,0},{7,1},{0,2},{1,3},{2,4},{3,5},{4,6},{5,7},{14,8},{15,9},{8,1... | collective-permute-start | bytes 589832 | tf_op jit(solution)/shard_map/ppermute | solution.py:29
  130.6 12.4 %collective-permute-start.36 = (bf16[64,1536]{1,0:T(8,128)(2,1)S(1)}, bf16[64,1536]{1,0:T(8,128)(2,1)S(1)}, u32[]{:S(2)}, u32[]{:S(2)}) collective-permute-start(bf16[64,1536]{1,0:T(8,128)(2,1)S(1)} %get-tuple-element.51), channel_id=1, source_target_pairs={{2,0},{3,1},{4,2},{5,3},{6,4},{7,5},{0,6},{1,7},{10,8},{11,9},{12,... | collective-permute-start | bytes 589832 | tf_op jit(solution)/shard_map/ppermute | solution.py:29
  135.2 14.4 %collective-permute-start.38 = (bf16[64,1536]{1,0:T(8,128)(2,1)S(1)}, bf16[64,1536]{1,0:T(8,128)(2,1)S(1)}, u32[]{:S(2)}, u32[]{:S(2)}) collective-permute-start(bf16[64,1536]{1,0:T(8,128)(2,1)S(1)} %get-tuple-element.53), channel_id=1, source_target_pairs={{1,0},{2,1},{3,2},{4,3},{5,4},{6,5},{7,6},{0,7},{9,8},{10,9},{11,1... | collective-permute-start | bytes 589832 | tf_op jit(solution)/shard_map/ppermute | solution.py:29
  137.2 31.4 %collective-permute-start.25 = (bf16[16,2688]{1,0:T(8,128)(2,1)S(1)}, bf16[16,2688]{1,0:T(8,128)(2,1)S(1)}, u32[]{:S(2)}, u32[]{:S(2)}) collective-permute-start(bf16[16,2688]{1,0:T(8,128)(2,1)S(1)} %get-tuple-element.38), channel_id=1, source_target_pairs={{4,0},{5,1},{6,2},{7,3},{0,4},{1,5},{2,6},{3,7},{12,8},{13,9},{14,... | collective-permute-start | bytes 258056 | tf_op jit(solution)/shard_map/ppermute | solution.py:29
  140.6 28.0 %collective-permute-start.26 = (bf16[16,2688]{1,0:T(8,128)(2,1)S(1)}, bf16[16,2688]{1,0:T(8,128)(2,1)S(1)}, u32[]{:S(2)}, u32[]{:S(2)}) collective-permute-start(bf16[16,2688]{1,0:T(8,128)(2,1)S(1)} %get-tuple-element.39), channel_id=1, source_target_pairs={{5,0},{6,1},{7,2},{0,3},{1,4},{2,5},{3,6},{4,7},{13,8},{14,9},{15,... | collective-permute-start | bytes 258056 | tf_op jit(solution)/shard_map/ppermute | solution.py:29
  150.5 25.3 %all-to-all-start.2 = ((bf16[32,2,1536]{2,1,0:T(2,128)(2,1)}), bf16[32,2,1536]{2,1,0:T(2,128)(2,1)S(1)}, u32[]{:S(2)}, u32[]{:S(2)}) async-start(bf16[32,2,1536]{2,1,0:T(2,128)(2,1)} %bitcast.4), calls=%async_computation.2 | async-start | bytes 393216 | tf_op jit(solution)/shard_map/all_to_all | solution.py:315
  162.9 13.0 %collective-permute-start.27 = (bf16[16,2688]{1,0:T(8,128)(2,1)S(1)}, bf16[16,2688]{1,0:T(8,128)(2,1)S(1)}, u32[]{:S(2)}, u32[]{:S(2)}) collective-permute-start(bf16[16,2688]{1,0:T(8,128)(2,1)S(1)} %get-tuple-element.40), channel_id=1, source_target_pairs={{3,0},{4,1},{5,2},{6,3},{7,4},{0,5},{1,6},{2,7},{11,8},{12,9},{13,... | collective-permute-start | bytes 258056 | tf_op jit(solution)/shard_map/ppermute | solution.py:29
  (22 other events, 408.2 us)
where the time goes:
time: 191 us
  starting transfers between devices  93.8 us (49%)
  waiting for transfers between devices  68.5 us (36%)
  Pallas kernels  10.9 us (6%)
  matrix products  10.8 us (6%)
  local copies, waits for them, and re-layouts  4.45 us (2%)
    ppermute x39, starting transfers between devices, pass_on(): lax.ppermute(value, axis, [((i + back) % peers, i) for i in range(peers)])  69.7 us
    ppermute x39, waiting for transfers between devices, pass_on(): lax.ppermute(value, axis, [((i + back) % peers, i) for i in range(peers)])  57.3 us
    all_to_all x1, starting transfers between devices, on_device(): lax.all_to_all(tiles_b.reshape(rows_y * owners, capacity, narrow), (Y, 'e...  12.3 us
    pallas_call x1, Pallas kernels, main_call(): pl.pallas_call(functools.partial(main_kernel, rows_y, rows_z, slots, len(...  9.17 us
    all_to_all x1, starting transfers between devices, on_device(): lax.all_to_all(send.reshape(owners, capacity, 2 * model_width), 'expert',...  6.51 us
    all_to_all x1, waiting for transfers between devices, on_device(): lax.all_to_all(send.reshape(owners, capacity, 2 * model_width), 'expert',...  6.49 us
    all_to_all x1, starting transfers between devices, on_device(): lax.all_to_all(slot_home.reshape(owners, capacity, wide), 'expert', 0, 0,...  5.22 us
    all_to_all x1, waiting for transfers between devices, on_device(): lax.all_to_all(slot_home.reshape(owners, capacity, wide), 'expert', 0, 0,...  4.73 us
  transfers between devices with their start and end apart: 42, of which 15 were waited for; matrix products, arithmetic and copies ran while one was open for 5% of the time, Pallas kernels for 1%

commit v1 on v0

--- a/solution.py
+++ b/solution.py
@@ -14,8 +14,9 @@
 Y = "replica_0"
 Z = "replica_1"
 LANES = 128
-SPLIT = 2560
+SPLIT = 2816
 CHUNK = 512
+STEP = 256
 VMEM = pl.BlockSpec(memory_space=pltpu.VMEM)
 SMEM = pl.BlockSpec(memory_space=pltpu.SMEM)
 LIMIT = pltpu.CompilerParams(vmem_limit_bytes=16 * 1024 * 1024)
@@ -27,10 +28,6 @@
 def pass_on(value, axis, back):
     peers = lax.axis_size(axis)
     return lax.ppermute(value, axis, [((i + back) % peers, i) for i in range(peers)])
-
-
-def direct(value, axis):
-    return [value] + [pass_on(value, axis, k) for k in range(1, lax.axis_size(axis))]
 
 
 def ring(value, axis, split=True):
@@ -68,7 +65,7 @@
     return jnp.sum(columns.astype(jnp.float32), axis=1, keepdims=True)
 
 
-def main_kernel(rows_y, rows_z, slots, count_t, count_s, *refs):
+def main_kernel(rows_y, rows_z, slots, count_t, count_s, place, *refs):
     token_refs, refs = refs[:count_t], refs[count_t:]
     scaled_refs, refs = refs[:count_s], refs[count_s:]
     wg, wu, wd, t_all, s_all, hid_s, gpg_t, upg_t = refs[:8]
@@ -106,7 +103,8 @@
     def middle(dz, carry):
         for dy in range(rows_y):
             here = pl.ds(pl.multiple_of((dy * rows_z + dz) * slots, slots), slots)
-            there = pl.ds(pl.multiple_of((dz * rows_y + dy) * slots, slots), slots)
+            at_y = lax.rem(place[0] + dy, rows_y)
+            there = pl.ds(pl.multiple_of((dz * rows_y + at_y) * slots, slots), slots)
             gate_pre = acc_g[here, :]
             up_pre = acc_u[here, :]
             hidden_grad = acc_h[there, :]
@@ -133,8 +131,8 @@
         rows = total // len(outs)
 
         def step_of(step, carry):
-            cols = pl.ds(pl.multiple_of(step * CHUNK, CHUNK), CHUNK)
-            wide = pl.ds(pl.multiple_of(step * CHUNK + shift, CHUNK), CHUNK)
+            cols = pl.ds(pl.multiple_of(step * STEP, STEP), STEP)
+            wide = pl.ds(pl.multiple_of(step * STEP + shift, STEP), STEP)
             value = (
                 jnp.dot(left[...], wg[:, wide], preferred_element_type=jnp.float32)
                 + jnp.dot(right[...], wu[:, wide], preferred_element_type=jnp.float32)
@@ -145,14 +143,14 @@
 
         return step_of
 
-    lax.fori_loop(0, SPLIT // CHUNK, slots_of(gpg_t, upg_t, out_a, 0), 0)
+    lax.fori_loop(0, SPLIT // STEP, slots_of(gpg_t, upg_t, out_a, 0), 0)
     for k, out in enumerate(out_a):
         rows = total // rows_y
         out[:, SPLIT:] = val_s[k * rows : (k + 1) * rows, :]
-    lax.fori_loop(0, (width - SPLIT) // CHUNK, slots_of(gpg_s, upg_s, out_b, SPLIT), 0)
-
-
-def main_call(token_blocks, scaled_blocks, wg, wu, wd, rows_y, rows_z, slots):
+    lax.fori_loop(0, (width - SPLIT) // STEP, slots_of(gpg_s, upg_s, out_b, SPLIT), 0)
+
+
+def main_call(place, token_blocks, scaled_blocks, wg, wu, wd, rows_y, rows_z, slots):
     total = rows_y * rows_z * slots
     hidden, width = wg.shape
     bf = jnp.bfloat16
@@ -166,7 +164,7 @@
             main_kernel, rows_y, rows_z, slots, len(token_blocks), len(scaled_blocks)
         ),
         out_shape=shapes,
-        in_specs=[VMEM] * (len(blocks) + 3),
+        in_specs=[SMEM] + [VMEM] * (len(blocks) + 3),
         out_specs=[VMEM] * len(shapes),
         scratch_shapes=[pltpu.VMEM((total, hidden), jnp.float32)] * 3
         + [pltpu.VMEM((total, LANES), bf)]
@@ -176,7 +174,7 @@
             flops=10 * total * hidden * width, bytes_accessed=30 << 20, transcendentals=0
         ),
         name="experts",
-    )(*blocks, wg, wu, wd)
+    )(place, *blocks, wg, wu, wd)
     return outs[:5], outs[5 : 5 + rows_y], outs[5 + rows_y :]
 
 
@@ -206,19 +204,18 @@
         add_narrow(ins, slice(k * slots, (k + 1) * slots), out)
 
 
-def sum_b_kernel(slots, place, *refs):
+def sum_b_kernel(slots, *refs):
     ins, out = refs[:-1], refs[-1]
     peers, owners, capacity = out.shape[0], out.shape[1], out.shape[2]
 
     def step(k, carry):
         rows = pl.ds(pl.multiple_of(k * slots, slots), slots)
-        target = lax.rem(place[0] + k, peers)
         total = ins[0][rows, :].astype(jnp.float32)
         for ref in ins[1:]:
             total = total + ref[rows, :].astype(jnp.float32)
         total = total.astype(jnp.bfloat16)
         for e in range(owners):
-            out[target, e] = total[e * capacity : (e + 1) * capacity]
+            out[k, e] = total[e * capacity : (e + 1) * capacity]
         return carry
 
     lax.fori_loop(0, peers, step, 0)
@@ -228,14 +225,14 @@
     ins, out = refs[:-1], refs[-1]
 
     def step(index, carry):
-        cols = pl.ds(pl.multiple_of(index * CHUNK, CHUNK), CHUNK)
+        cols = pl.ds(pl.multiple_of(index * STEP, STEP), STEP)
         total = ins[0][:, cols].astype(jnp.float32)
         for ref in ins[1:]:
             total = total + ref[:, cols].astype(jnp.float32)
         out[:, cols] = total.astype(jnp.bfloat16)
         return carry
 
-    lax.fori_loop(0, SPLIT // CHUNK, step, 0)
+    lax.fori_loop(0, SPLIT // STEP, step, 0)
     add_narrow(ins, slice(None), out)
 
 
@@ -263,32 +260,30 @@
     token_hot = token_hot.reshape(token_count, fan_out, slots)
     dispatch = jnp.sum(token_hot, axis=1).astype(bf)
     slot_gate = jnp.sum(token_hot * gates[:, :, None], axis=(0, 1))
-    picked = lax.dot_general(
-        dispatch,
-        jnp.concatenate([tokens, out_grad], axis=1),
-        LEADING,
-        preferred_element_type=jnp.float32,
-    )
-    scale = jnp.concatenate(
-        [
-            jnp.ones((slots, model_width), jnp.float32),
-            jnp.broadcast_to(slot_gate[:, None], (slots, model_width)),
-        ],
-        axis=1,
-    )
-    send = (picked * scale).astype(bf)
+    send_tokens = lax.dot_general(dispatch, tokens, LEADING, preferred_element_type=jnp.float32)
+    send_scaled = slot_gate[:, None] * lax.dot_general(
+        dispatch, out_grad, LEADING, preferred_element_type=jnp.float32
+    )
     owned = lax.all_to_all(
-        send.reshape(owners, capacity, 2 * model_width), "expert", 0, 0, tiled=True
-    ).reshape(slots, 2 * model_width)
-    owned, place = lax.optimization_barrier((owned, lax.axis_index(Y).reshape(1)))
-    scaled_y = jnp.concatenate(direct(owned[:, model_width:], Y), axis=0)
-    tokens_z = jnp.concatenate(
-        ring(owned[:, :model_width], Z, split=False), axis=0
-    )
+        send_tokens.astype(bf).reshape(owners, capacity, model_width),
+        "expert",
+        0,
+        0,
+        tiled=True,
+    ).reshape(slots, model_width)
+    copies = jnp.broadcast_to(
+        send_scaled.astype(bf).reshape(1, owners, capacity, model_width),
+        (rows_y, owners, capacity, model_width),
+    ).reshape(rows_y * owners, capacity, model_width)
+    copies, place = lax.optimization_barrier((copies, lax.axis_index(Y).reshape(1)))
+    scaled_y = lax.all_to_all(copies, (Y, "expert"), 0, 0, tiled=True).reshape(
+        rows_y * slots, model_width
+    )
+    tokens_z = jnp.concatenate(ring(owned, Z, split=False), axis=0)
     token_blocks = ring(tokens_z, Y)
     scaled_blocks = ring(scaled_y, Z)
     (gathered, scaled, hidden, gate_pre_grad, up_pre_grad), out_a, out_b = main_call(
-        token_blocks, scaled_blocks, w_gate[0], w_up[0], w_down[0], rows_y, rows_z, slots
+        place, token_blocks, scaled_blocks, w_gate[0], w_up[0], w_down[0], rows_y, rows_z, slots
     )
     arrived_b = [pass_on(out_b[k], Z, -k) for k in far_first(rows_z)]
     arrived_a = [pass_on(out_a[k], Y, -k) for k in range(1, rows_y)]
@@ -306,12 +301,12 @@
     tiles_b = pl.pallas_call(
         functools.partial(sum_b_kernel, slots),
         out_shape=jax.ShapeDtypeStruct((rows_y, owners, capacity, narrow), bf),
-        in_specs=[SMEM] + [VMEM] * rows_z,
+        in_specs=[VMEM] * rows_z,
         out_specs=VMEM,
         compiler_params=SMALL,
         cost_estimate=cost(rows_y * rows_z * slots * narrow),
         name="sum_z",
-    )(place, out_b[0], *arrived_b)
+    )(out_b[0], *arrived_b)
     back_b = lax.all_to_all(
         tiles_b.reshape(rows_y * owners, capacity, narrow), (Y, "expert"), 0, 0, tiled=True
     ).reshape(rows_y * slots, narrow)

time: 191 us -> 196 us (1.026)
  local copies, waits for them, and re-layouts: 4.45 us -> 10.3 us
  waiting for transfers between devices: 68.5 us -> 63.3 us
  starting transfers between devices: 93.8 us -> 96 us
    all_to_all x1 -> x2, starting transfers between devices: 6.51 us -> 11.9 us  [the longest x1 6.47 us: on_device(): lax.all_to_all(send_tokens.astype(bf).reshape(owners, capacity, model_wid...]
    unnamed x17 -> x20, local copies, waits for them, and re-layouts: 2.28 us -> 6.8 us
    all_to_all x1 -> x2, waiting for transfers between devices: 6.49 us -> 2.8 us  [the longest x1 2.8 us: on_device(): lax.all_to_all(send_tokens.astype(bf).reshape(owners, capacity, model_wid...]
    ppermute x39 -> x36, starting transfers between devices: 69.7 us -> 67.1 us  [pass_on(): lax.ppermute(value, axis, [((i + back) % peers, i) for i in range(peers)])]
    ppermute x39 -> x36, waiting for transfers between devices: 57.3 us -> 55.7 us  [pass_on(): lax.ppermute(value, axis, [((i + back) % peers, i) for i in range(peers)])]
  transfers between devices with their start and end apart: 42 -> 40, of which waited for: 15 -> 11; matrix products, arithmetic and copies ran while one was open for 5% -> 6% of each run, Pallas kernels for 1% -> 1%
where the time goes in v1:
time: 196 us; the launch traced here: 195 us
  starting transfers between devices  96 us (49%)
  waiting for transfers between devices  63.3 us (32%)
  Pallas kernels  12.4 us (6%)
  matrix products  10.9 us (6%)
  local copies, waits for them, and re-layouts  10.3 us (5%)
    ppermute x36, starting transfers between devices, pass_on(): lax.ppermute(value, axis, [((i + back) % peers, i) for i in range(peers)])  67.1 us
    ppermute x36, waiting for transfers between devices, pass_on(): lax.ppermute(value, axis, [((i + back) % peers, i) for i in range(peers)])  55.7 us
    all_to_all x1, starting transfers between devices, on_device(): lax.all_to_all(tiles_b.reshape(rows_y * owners, capacity, narrow), (Y, 'e...  11.6 us
    pallas_call x1, Pallas kernels, main_call(): pl.pallas_call(functools.partial(main_kernel, rows_y, rows_z, slots, len(...  10.6 us
    unnamed x20, local copies, waits for them, and re-layouts  6.8 us
    all_to_all x1, starting transfers between devices, on_device(): lax.all_to_all(send_tokens.astype(bf).reshape(owners, capacity, model_wid...  6.47 us
    all_to_all x1, starting transfers between devices, on_device(): lax.all_to_all(slot_home.reshape(owners, capacity, wide), 'expert', 0, 0,...  5.42 us
    all_to_all x1, starting transfers between devices, on_device(): lax.all_to_all(copies, (Y, 'expert'), 0, 0, tiled=True)  5.38 us
  transfers between devices with their start and end apart: 40, of which 11 were waited for; matrix products, arithmetic and copies ran while one was open for 6% of the time, Pallas kernels for 1%

profile of v1, /device:TPU:1, one launch (start us, length us, event | category | flops | bytes accessed | tf_op | source)
XLA Modules:
  0.0 195.0 jit_solution(5150598643067259521)
XLA Ops:
  3.7 6.5 %all-to-all-start = ((bf16[8,2,4096]{2,1,0:T(2,128)(2,1)}), bf16[8,2,4096]{2,1,0:T(2,128)(2,1)S(1)}, u32[]{:S(2)}, u32[]{:S(2)}) async-start(bf16[8,2,4096]{2,1,0:T(2,128)(2,1)} %reshape.64), calls=%async_computation | async-start | bytes 262144 | tf_op jit(solution)/shard_map/all_to_all | solution.py:267
  12.6 2.8 %all-to-all-done = bf16[8,2,4096]{2,1,0:T(2,128)(2,1)S(1)} async-done(((bf16[8,2,4096]{2,1,0:T(2,128)(2,1)}), bf16[8,2,4096]{2,1,0:T(2,128)(2,1)S(1)}, u32[]{:S(2)}, u32[]{:S(2)}) %all-to-all-start) | async-done | bytes 131104 | tf_op jit(solution)/shard_map/all_to_all | solution.py:267
  15.4 5.4 %all-to-all-start.1 = ((bf16[32,2,4096]{2,1,0:T(2,128)(2,1)}), bf16[32,2,4096]{2,1,0:T(2,128)(2,1)S(1)}, u32[]{:S(2)}, u32[]{:S(2)}) async-start(bf16[32,2,4096]{2,1,0:T(2,128)(2,1)} %bitcast), calls=%async_computation.1 | async-start | bytes 1048576 | tf_op jit(solution)/shard_map/all_to_all | solution.py:279
  22.6 4.0 %collective-permute-start = (bf16[16,4096]{1,0:T(8,128)(2,1)S(1)}, bf16[16,4096]{1,0:T(8,128)(2,1)S(1)}, u32[]{:S(2)}, u32[]{:S(2)}) collective-permute-start(bf16[16,4096]{1,0:T(8,128)(2,1)S(1)} %reshape.65), channel_id=1, source_target_pairs={{1,0},{2,1},{3,2},{4,3},{5,4},{6,5},{7,6},{0,7},{9,8},{10,9},{11,1... | collective-permute-start | bytes 393224 | tf_op jit(solution)/shard_map/ppermute | solution.py:30
  26.6 3.5 %collective-permute-done.4 = bf16[16,4096]{1,0:T(8,128)(2,1)S(1)} collective-permute-done((bf16[16,4096]{1,0:T(8,128)(2,1)S(1)}, bf16[16,4096]{1,0:T(8,128)(2,1)S(1)}, u32[]{:S(2)}, u32[]{:S(2)}) %collective-permute-start.4) | collective-permute-done | bytes 131104 | tf_op jit(solution)/shard_map/ppermute | solution.py:30
  43.3 11.2 %collective-permute-done.3 = bf16[16,4096]{1,0:T(8,128)(2,1)S(1)} collective-permute-done((bf16[16,4096]{1,0:T(8,128)(2,1)S(1)}, bf16[16,4096]{1,0:T(8,128)(2,1)S(1)}, u32[]{:S(2)}, u32[]{:S(2)}) %collective-permute-start.3) | collective-permute-done | bytes 131104 | tf_op jit(solution)/shard_map/ppermute | solution.py:30
  57.4 3.5 %collective-permute-start.12 = (bf16[64,4096]{1,0:T(8,128)(2,1)S(1)}, bf16[64,4096]{1,0:T(8,128)(2,1)S(1)}, u32[]{:S(2)}, u32[]{:S(2)}) collective-permute-start(bf16[64,4096]{1,0:T(8,128)(2,1)S(1)} %collective-permute-done.11.refs_6_), channel_id=1, source_target_pairs={{1,0},{2,1},{3,2},{4,3},{5,4},{6,5},{7,6},{0,7},{9,8},{10,9},{11,1... | collective-permute-start | bytes 1572872 | tf_op jit(solution)/shard_map/ppermute | solution.py:30
  60.8 9.1 %collective-permute-done.16.refs_12_ = bf16[64,4096]{1,0:T(8,128)(2,1)S(1)} collective-permute-done((bf16[64,4096]{1,0:T(8,128)(2,1)S(1)}, bf16[64,4096]{1,0:T(8,128)(2,1)S(1)}, u32[]{:S(2)}, u32[]{:S(2)}) %collective-permute-start.16) | collective-permute-done | bytes 524320 | tf_op jit(solution)/shard_map/ppermute | solution.py:30
  72.6 5.4 %collective-permute-done.9.refs_4_ = bf16[128,4096]{1,0:T(8,128)(2,1)S(1)} collective-permute-done((bf16[128,4096]{1,0:T(8,128)(2,1)S(1)}, bf16[128,4096]{1,0:T(8,128)(2,1)S(1)}, u32[]{:S(2)}, u32[]{:S(2)}) %collective-permute-start.9) | collective-permute-done | bytes 1048608 | tf_op jit(solution)/shard_map/ppermute | solution.py:30
  81.1 3.5 %collective-permute-start.14 = (bf16[32,4096]{1,0:T(8,128)(2,1)S(1)}, bf16[32,4096]{1,0:T(8,128)(2,1)S(1)}, u32[]{:S(2)}, u32[]{:S(2)}) collective-permute-start(bf16[32,4096]{1,0:T(8,128)(2,1)S(1)} %slice.26), channel_id=1, source_target_pairs={{1,0},{2,1},{3,2},{4,3},{5,4},{6,5},{7,6},{0,7},{9,8},{10,9},{11,1... | collective-permute-start | bytes 786440 | tf_op jit(solution)/shard_map/ppermute | solution.py:30
  84.6 4.9 %collective-permute-done.10.refs_3_ = bf16[64,4096]{1,0:T(8,128)(2,1)S(1)} collective-permute-done((bf16[64,4096]{1,0:T(8,128)(2,1)S(1)}, bf16[64,4096]{1,0:T(8,128)(2,1)S(1)}, u32[]{:S(2)}, u32[]{:S(2)}) %collective-permute-start.10) | collective-permute-done | bytes 524320 | tf_op jit(solution)/shard_map/ppermute | solution.py:30
  94.0 10.6 %experts.1 = (bf16[512,4096]{1,0:T(8,128)(2,1)S(1)}, bf16[512,4096]{1,0:T(8,128)(2,1)S(1)}, bf16[512,224]{1,0:T(8,128)(2,1)S(1)}, bf16[512,224]{1,0:T(8,128)(2,1...) custom-call(s32[1]{0:T(128)} %bitcast.1.place, ...), custom_call_target="tpu_custom_call" | custom-call | flops 4697620480 | bytes 31457280 | tf_op jit(solution)/shard_map/experts/pallas_call | solution.py:162
  104.7 3.7 %collective-permute-start.20 = (bf16[128,2944]{1,0:T(8,128)(2,1)S(1)}, bf16[128,2944]{1,0:T(8,128)(2,1)S(1)}, u32[]{:S(2)}, u32[]{:S(2)}) collective-permute-start(bf16[128,2944]{1,0:T(8,128)(2,1)S(1)} %get-tuple-element.36), channel_id=1, source_target_pairs={{16,0},{24,8},{0,16},{8,24},{17,1},{25,9},{1,17},{9,25},{18,2},{26... | collective-permute-start | bytes 2261000 | tf_op jit(solution)/shard_map/ppermute | solution.py:30
  108.4 3.9 %collective-permute-start.29 = (bf16[64,1280]{1,0:T(8,128)(2,1)S(1)}, bf16[64,1280]{1,0:T(8,128)(2,1)S(1)}, u32[]{:S(2)}, u32[]{:S(2)}) collective-permute-start(bf16[64,1280]{1,0:T(8,128)(2,1)S(1)} %get-tuple-element.47), channel_id=1, source_target_pairs={{4,0},{5,1},{6,2},{7,3},{0,4},{1,5},{2,6},{3,7},{12,8},{13,9},{14,... | collective-permute-start | bytes 491528 | tf_op jit(solution)/shard_map/ppermute | solution.py:30
  114.8 5.3 %collective-permute-done.19.refs_1_ = bf16[128,2944]{1,0:T(8,128)(2,1)S(1)} collective-permute-done((bf16[128,2944]{1,0:T(8,128)(2,1)S(1)}, bf16[128,2944]{1,0:T(8,128)(2,1)S(1)}, u32[]{:S(2)}, u32[]{:S(2)}) %collective-permute-start.19) | collective-permute-done | bytes 753696 | tf_op jit(solution)/shard_map/ppermute | solution.py:30
  120.0 4.2 %collective-permute-start.31 = (bf16[64,1280]{1,0:T(8,128)(2,1)S(1)}, bf16[64,1280]{1,0:T(8,128)(2,1)S(1)}, u32[]{:S(2)}, u32[]{:S(2)}) collective-permute-start(bf16[64,1280]{1,0:T(8,128)(2,1)S(1)} %get-tuple-element.49), channel_id=1, source_target_pairs={{3,0},{4,1},{5,2},{6,3},{7,4},{0,5},{1,6},{2,7},{11,8},{12,9},{13,... | collective-permute-start | bytes 491528 | tf_op jit(solution)/shard_map/ppermute | solution.py:30
  124.2 12.7 %collective-permute-done.20.refs_2_ = bf16[128,2944]{1,0:T(8,128)(2,1)S(1)} collective-permute-done((bf16[128,2944]{1,0:T(8,128)(2,1)S(1)}, bf16[128,2944]{1,0:T(8,128)(2,1)S(1)}, u32[]{:S(2)}, u32[]{:S(2)}) %collective-permute-start.20) | collective-permute-done | bytes 753696 | tf_op jit(solution)/shard_map/ppermute | solution.py:30
  146.5 3.9 %collective-permute-start.22 = (bf16[16,2944]{1,0:T(8,128)(2,1)S(1)}, bf16[16,2944]{1,0:T(8,128)(2,1)S(1)}, u32[]{:S(2)}, u32[]{:S(2)}) collective-permute-start(bf16[16,2944]{1,0:T(8,128)(2,1)S(1)} %get-tuple-element.39), channel_id=1, source_target_pairs={{4,0},{5,1},{6,2},{7,3},{0,4},{1,5},{2,6},{3,7},{12,8},{13,9},{14,... | collective-permute-start | bytes 282632 | tf_op jit(solution)/shard_map/ppermute | solution.py:30
  153.8 11.6 %all-to-all-start.3 = ((bf16[32,2,1280]{2,1,0:T(2,128)(2,1)}), bf16[32,2,1280]{2,1,0:T(2,128)(2,1)S(1)}, u32[]{:S(2)}, u32[]{:S(2)}) async-start(bf16[32,2,1280]{2,1,0:T(2,128)(2,1)} %bitcast.5), calls=%async_computation.3 | async-start | bytes 327680 | tf_op jit(solution)/shard_map/all_to_all | solution.py:310
  165.4 4.8 %collective-permute-start.24 = (bf16[16,2944]{1,0:T(8,128)(2,1)S(1)}, bf16[16,2944]{1,0:T(8,128)(2,1)S(1)}, u32[]{:S(2)}, u32[]{:S(2)}) collective-permute-start(bf16[16,2944]{1,0:T(8,128)(2,1)S(1)} %get-tuple-element.41), channel_id=1, source_target_pairs={{3,0},{4,1},{5,2},{6,3},{7,4},{0,5},{1,6},{2,7},{11,8},{12,9},{13,... | collective-permute-start | bytes 282632 | tf_op jit(solution)/shard_map/ppermute | solution.py:30
  170.2 3.6 %collective-permute-start.26 = (bf16[16,2944]{1,0:T(8,128)(2,1)S(1)}, bf16[16,2944]{1,0:T(8,128)(2,1)S(1)}, u32[]{:S(2)}, u32[]{:S(2)}) collective-permute-start(bf16[16,2944]{1,0:T(8,128)(2,1)S(1)} %get-tuple-element.43), channel_id=1, source_target_pairs={{2,0},{3,1},{4,2},{5,3},{6,4},{7,5},{0,6},{1,7},{10,8},{11,9},{12,... | collective-permute-start | bytes 282632 | tf_op jit(solution)/shard_map/ppermute | solution.py:30
  176.5 4.6 %fusion.2 = bf16[1,224,4096]{2,1,0:T(8,128)(2,1)} fusion(bf16[512,224]{1,0:T(8,128)(2,1)S(1)} %get-tuple-element.57, bf16[512,4096]{1,0:T(8,128)(2,1)} %copy-done.1), kind=kOutput, calls=%fused_computation.5 | convolution fusion | flops 940441600 | bytes 6258688 | tf_op jit(solution)/shard_map/dot_general | solution.py:290
  182.9 5.4 %all-to-all-start.2 = ((bf16[8,2,2944]{2,1,0:T(2,128)(2,1)}), bf16[8,2,2944]{2,1,0:T(2,128)(2,1)S(1)}, u32[]{:S(2)}, u32[]{:S(2)}) async-start(bf16[8,2,2944]{2,1,0:T(2,128)(2,1)} %reshape.67), calls=%async_computation.2 | async-start | bytes 188416 | tf_op jit(solution)/shard_map/all_to_all | solution.py:332
  188.5 4.8 %all-to-all-done.2 = bf16[8,2,2944]{2,1,0:T(2,128)(2,1)S(1)} async-done(((bf16[8,2,2944]{2,1,0:T(2,128)(2,1)}), bf16[8,2,2944]{2,1,0:T(2,128)(2,1)S(1)}, u32[]{:S(2)}, u32[]{:S(2)}) %all-to-all-start.2) | async-done | bytes 94240 | tf_op jit(solution)/shard_map/all_to_all | solution.py:332
  (109 shorter events, 55.4 us)
Async XLA Ops:
  3.7 11.7 %all-to-all-start = ((bf16[8,2,4096]{2,1,0:T(2,128)(2,1)}), bf16[8,2,4096]{2,1,0:T(2,128)(2,1)S(1)}, u32[]{:S(2)}, u32[]{:S(2)}) async-start(bf16[8,2,4096]{2,1,0:T(2,128)(2,1)} %reshape.64), calls=%async_computation | async-start | bytes 262144 | tf_op jit(solution)/shard_map/all_to_all | solution.py:267
  15.4 22.9 %all-to-all-start.1 = ((bf16[32,2,4096]{2,1,0:T(2,128)(2,1)}), bf16[32,2,4096]{2,1,0:T(2,128)(2,1)S(1)}, u32[]{:S(2)}, u32[]{:S(2)}) async-start(bf16[32,2,4096]{2,1,0:T(2,128)(2,1)} %bitcast), calls=%async_computation.1 | async-start | bytes 1048576 | tf_op jit(solution)/shard_map/all_to_all | solution.py:279
  35.6 18.9 %collective-permute-start.6 = (bf16[16,4096]{1,0:T(8,128)(2,1)S(1)}, bf16[16,4096]{1,0:T(8,128)(2,1)S(1)}, u32[]{:S(2)}, u32[]{:S(2)}) collective-permute-start(bf16[16,4096]{1,0:T(8,128)(2,1)S(1)} %collective-permute-done.5), channel_id=1, source_target_pairs={{7,0},{0,1},{1,2},{2,3},{3,4},{4,5},{5,6},{6,7},{15,8},{8,9},{9,10... | collective-permute-start | bytes 393224 | tf_op jit(solution)/shard_map/ppermute | solution.py:30
  38.5 18.8 %collective-permute-start.15 = (bf16[64,4096]{1,0:T(8,128)(2,1)S(1)}, bf16[64,4096]{1,0:T(8,128)(2,1)S(1)}, u32[]{:S(2)}, u32[]{:S(2)}) collective-permute-start(bf16[64,4096]{1,0:T(8,128)(2,1)S(1)} %reshape.66.refs_5_), channel_id=1, source_target_pairs={{7,0},{0,1},{1,2},{2,3},{3,4},{4,5},{5,6},{6,7},{15,8},{8,9},{9,10... | collective-permute-start | bytes 1572872 | tf_op jit(solution)/shard_map/ppermute | solution.py:30
  38.6 18.7 %collective-permute-start.11 = (bf16[64,4096]{1,0:T(8,128)(2,1)S(1)}, bf16[64,4096]{1,0:T(8,128)(2,1)S(1)}, u32[]{:S(2)}, u32[]{:S(2)}) collective-permute-start(bf16[64,4096]{1,0:T(8,128)(2,1)S(1)} %reshape.66.refs_5_), channel_id=1, source_target_pairs={{1,0},{2,1},{3,2},{4,3},{5,4},{6,5},{7,6},{0,7},{9,8},{10,9},{11,1... | collective-permute-start | bytes 1572872 | tf_op jit(solution)/shard_map/ppermute | solution.py:30
  41.3 13.2 %collective-permute-start.3 = (bf16[16,4096]{1,0:T(8,128)(2,1)S(1)}, bf16[16,4096]{1,0:T(8,128)(2,1)S(1)}, u32[]{:S(2)}, u32[]{:S(2)}) collective-permute-start(bf16[16,4096]{1,0:T(8,128)(2,1)S(1)} %collective-permute-done.2), channel_id=1, source_target_pairs={{1,0},{2,1},{3,2},{4,3},{5,4},{6,5},{7,6},{0,7},{9,8},{10,9},{11,1... | collective-permute-start | bytes 393224 | tf_op jit(solution)/shard_map/ppermute | solution.py:30
  54.6 23.5 %collective-permute-start.9 = (bf16[128,4096]{1,0:T(8,128)(2,1)S(1)}, bf16[128,4096]{1,0:T(8,128)(2,1)S(1)}, u32[]{:S(2)}, u32[]{:S(2)}) collective-permute-start(bf16[128,4096]{1,0:T(8,128)(2,1)S(1)} %constant_dynamic-update-slice_fusion.refs_0_), channel_id=1, source_target_pairs={{24,0},{0,8},{8,16},{16,24},{25,1},{1,9},{9,17},{17,25},{26,2},{2,... | collective-permute-start | bytes 3145736 | tf_op jit(solution)/shard_map/ppermute | solution.py:30
  55.9 22.3 %collective-permute-start.7 = (bf16[128,4096]{1,0:T(8,128)(2,1)S(1)}, bf16[128,4096]{1,0:T(8,128)(2,1)S(1)}, u32[]{:S(2)}, u32[]{:S(2)}) collective-permute-start(bf16[128,4096]{1,0:T(8,128)(2,1)S(1)} %constant_dynamic-update-slice_fusion.refs_0_), channel_id=1, source_target_pairs={{8,0},{16,8},{24,16},{0,24},{9,1},{17,9},{25,17},{1,25},{10,2},{18... | collective-permute-start | bytes 3145736 | tf_op jit(solution)/shard_map/ppermute | solution.py:30
  57.4 12.6 %collective-permute-start.16 = (bf16[64,4096]{1,0:T(8,128)(2,1)S(1)}, bf16[64,4096]{1,0:T(8,128)(2,1)S(1)}, u32[]{:S(2)}, u32[]{:S(2)}) collective-permute-start(bf16[64,4096]{1,0:T(8,128)(2,1)S(1)} %collective-permute-done.15.refs_13_), channel_id=1, source_target_pairs={{7,0},{0,1},{1,2},{2,3},{3,4},{4,5},{5,6},{6,7},{15,8},{8,9},{9,10... | collective-permute-start | bytes 1572872 | tf_op jit(solution)/shard_map/ppermute | solution.py:30
  57.4 12.6 %collective-permute-start.12 = (bf16[64,4096]{1,0:T(8,128)(2,1)S(1)}, bf16[64,4096]{1,0:T(8,128)(2,1)S(1)}, u32[]{:S(2)}, u32[]{:S(2)}) collective-permute-start(bf16[64,4096]{1,0:T(8,128)(2,1)S(1)} %collective-permute-done.11.refs_6_), channel_id=1, source_target_pairs={{1,0},{2,1},{3,2},{4,3},{5,4},{6,5},{7,6},{0,7},{9,8},{10,9},{11,1... | collective-permute-start | bytes 1572872 | tf_op jit(solution)/shard_map/ppermute | solution.py:30
  78.1 11.4 %collective-permute-start.10 = (bf16[64,4096]{1,0:T(8,128)(2,1)S(1)}, bf16[64,4096]{1,0:T(8,128)(2,1)S(1)}, u32[]{:S(2)}, u32[]{:S(2)}) collective-permute-start(bf16[64,4096]{1,0:T(8,128)(2,1)S(1)} %slice.25), channel_id=1, source_target_pairs={{24,0},{0,8},{8,16},{16,24},{25,1},{1,9},{9,17},{17,25},{26,2},{2,... | collective-permute-start | bytes 1572872 | tf_op jit(solution)/shard_map/ppermute | solution.py:30
  78.2 11.2 %collective-permute-start.8 = (bf16[64,4096]{1,0:T(8,128)(2,1)S(1)}, bf16[64,4096]{1,0:T(8,128)(2,1)S(1)}, u32[]{:S(2)}, u32[]{:S(2)}) collective-permute-start(bf16[64,4096]{1,0:T(8,128)(2,1)S(1)} %slice.24), channel_id=1, source_target_pairs={{8,0},{16,8},{24,16},{0,24},{9,1},{17,9},{25,17},{1,25},{10,2},{18... | collective-permute-start | bytes 1572872 | tf_op jit(solution)/shard_map/ppermute | solution.py:30
  104.6 15.4 %collective-permute-start.19 = (bf16[128,2944]{1,0:T(8,128)(2,1)S(1)}, bf16[128,2944]{1,0:T(8,128)(2,1)S(1)}, u32[]{:S(2)}, u32[]{:S(2)}) collective-permute-start(bf16[128,2944]{1,0:T(8,128)(2,1)S(1)} %get-tuple-element.35), channel_id=1, source_target_pairs={{24,0},{0,8},{8,16},{16,24},{25,1},{1,9},{9,17},{17,25},{26,2},{2,... | collective-permute-start | bytes 2261000 | tf_op jit(solution)/shard_map/ppermute | solution.py:30
  104.7 32.2 %collective-permute-start.20 = (bf16[128,2944]{1,0:T(8,128)(2,1)S(1)}, bf16[128,2944]{1,0:T(8,128)(2,1)S(1)}, u32[]{:S(2)}, u32[]{:S(2)}) collective-permute-start(bf16[128,2944]{1,0:T(8,128)(2,1)S(1)} %get-tuple-element.36), channel_id=1, source_target_pairs={{16,0},{24,8},{0,16},{8,24},{17,1},{25,9},{1,17},{9,25},{18,2},{26... | collective-permute-start | bytes 2261000 | tf_op jit(solution)/shard_map/ppermute | solution.py:30
  108.4 33.2 %collective-permute-start.21 = (bf16[128,2944]{1,0:T(8,128)(2,1)S(1)}, bf16[128,2944]{1,0:T(8,128)(2,1)S(1)}, u32[]{:S(2)}, u32[]{:S(2)}) collective-permute-start(bf16[128,2944]{1,0:T(8,128)(2,1)S(1)} %get-tuple-element.37), channel_id=1, source_target_pairs={{8,0},{16,8},{24,16},{0,24},{9,1},{17,9},{25,17},{1,25},{10,2},{18... | collective-permute-start | bytes 2261000 | tf_op jit(solution)/shard_map/ppermute | solution.py:30
  108.4 35.2 %collective-permute-start.29 = (bf16[64,1280]{1,0:T(8,128)(2,1)S(1)}, bf16[64,1280]{1,0:T(8,128)(2,1)S(1)}, u32[]{:S(2)}, u32[]{:S(2)}) collective-permute-start(bf16[64,1280]{1,0:T(8,128)(2,1)S(1)} %get-tuple-element.47), channel_id=1, source_target_pairs={{4,0},{5,1},{6,2},{7,3},{0,4},{1,5},{2,6},{3,7},{12,8},{13,9},{14,... | collective-permute-start | bytes 491528 | tf_op jit(solution)/shard_map/ppermute | solution.py:30
  112.2 33.7 %collective-permute-start.30 = (bf16[64,1280]{1,0:T(8,128)(2,1)S(1)}, bf16[64,1280]{1,0:T(8,128)(2,1)S(1)}, u32[]{:S(2)}, u32[]{:S(2)}) collective-permute-start(bf16[64,1280]{1,0:T(8,128)(2,1)S(1)} %get-tuple-element.48), channel_id=1, source_target_pairs={{5,0},{6,1},{7,2},{0,3},{1,4},{2,5},{3,6},{4,7},{13,8},{14,9},{15,... | collective-permute-start | bytes 491528 | tf_op jit(solution)/shard_map/ppermute | solution.py:30
  120.0 26.5 %collective-permute-start.31 = (bf16[64,1280]{1,0:T(8,128)(2,1)S(1)}, bf16[64,1280]{1,0:T(8,128)(2,1)S(1)}, u32[]{:S(2)}, u32[]{:S(2)}) collective-permute-start(bf16[64,1280]{1,0:T(8,128)(2,1)S(1)} %get-tuple-element.49), channel_id=1, source_target_pairs={{3,0},{4,1},{5,2},{6,3},{7,4},{0,5},{1,6},{2,7},{11,8},{12,9},{13,... | collective-permute-start | bytes 491528 | tf_op jit(solution)/shard_map/ppermute | solution.py:30
  136.9 13.5 %collective-permute-start.32 = (bf16[64,1280]{1,0:T(8,128)(2,1)S(1)}, bf16[64,1280]{1,0:T(8,128)(2,1)S(1)}, u32[]{:S(2)}, u32[]{:S(2)}) collective-permute-start(bf16[64,1280]{1,0:T(8,128)(2,1)S(1)} %get-tuple-element.50), channel_id=1, source_target_pairs={{6,0},{7,1},{0,2},{1,3},{2,4},{3,5},{4,6},{5,7},{14,8},{15,9},{8,1... | collective-permute-start | bytes 491528 | tf_op jit(solution)/shard_map/ppermute | solution.py:30
  141.5 11.4 %collective-permute-start.33 = (bf16[64,1280]{1,0:T(8,128)(2,1)S(1)}, bf16[64,1280]{1,0:T(8,128)(2,1)S(1)}, u32[]{:S(2)}, u32[]{:S(2)}) collective-permute-start(bf16[64,1280]{1,0:T(8,128)(2,1)S(1)} %get-tuple-element.51), channel_id=1, source_target_pairs={{2,0},{3,1},{4,2},{5,3},{6,4},{7,5},{0,6},{1,7},{10,8},{11,9},{12,... | collective-permute-start | bytes 491528 | tf_op jit(solution)/shard_map/ppermute | solution.py:30
  146.5 27.3 %collective-permute-start.22 = (bf16[16,2944]{1,0:T(8,128)(2,1)S(1)}, bf16[16,2944]{1,0:T(8,128)(2,1)S(1)}, u32[]{:S(2)}, u32[]{:S(2)}) collective-permute-start(bf16[16,2944]{1,0:T(8,128)(2,1)S(1)} %get-tuple-element.39), channel_id=1, source_target_pairs={{4,0},{5,1},{6,2},{7,3},{0,4},{1,5},{2,6},{3,7},{12,8},{13,9},{14,... | collective-permute-start | bytes 282632 | tf_op jit(solution)/shard_map/ppermute | solution.py:30
  150.4 23.4 %collective-permute-start.23 = (bf16[16,2944]{1,0:T(8,128)(2,1)S(1)}, bf16[16,2944]{1,0:T(8,128)(2,1)S(1)}, u32[]{:S(2)}, u32[]{:S(2)}) collective-permute-start(bf16[16,2944]{1,0:T(8,128)(2,1)S(1)} %get-tuple-element.40), channel_id=1, source_target_pairs={{5,0},{6,1},{7,2},{0,3},{1,4},{2,5},{3,6},{4,7},{13,8},{14,9},{15,... | collective-permute-start | bytes 282632 | tf_op jit(solution)/shard_map/ppermute | solution.py:30
  153.8 27.2 %all-to-all-start.3 = ((bf16[32,2,1280]{2,1,0:T(2,128)(2,1)}), bf16[32,2,1280]{2,1,0:T(2,128)(2,1)S(1)}, u32[]{:S(2)}, u32[]{:S(2)}) async-start(bf16[32,2,1280]{2,1,0:T(2,128)(2,1)} %bitcast.5), calls=%async_computation.3 | async-start | bytes 327680 | tf_op jit(solution)/shard_map/all_to_all | solution.py:310
  165.4 15.7 %collective-permute-start.24 = (bf16[16,2944]{1,0:T(8,128)(2,1)S(1)}, bf16[16,2944]{1,0:T(8,128)(2,1)S(1)}, u32[]{:S(2)}, u32[]{:S(2)}) collective-permute-start(bf16[16,2944]{1,0:T(8,128)(2,1)S(1)} %get-tuple-element.41), channel_id=1, source_target_pairs={{3,0},{4,1},{5,2},{6,3},{7,4},{0,5},{1,6},{2,7},{11,8},{12,9},{13,... | collective-permute-start | bytes 282632 | tf_op jit(solution)/shard_map/ppermute | solution.py:30
  (21 other events, 179.9 us)

commit v2 on v1

--- a/solution.py
+++ b/solution.py
@@ -14,9 +14,9 @@
 Y = "replica_0"
 Z = "replica_1"
 LANES = 128
-SPLIT = 2816
+SPLIT = 2560
 CHUNK = 512
-STEP = 256
+STEP = 512
 VMEM = pl.BlockSpec(memory_space=pltpu.VMEM)
 SMEM = pl.BlockSpec(memory_space=pltpu.SMEM)
 LIMIT = pltpu.CompilerParams(vmem_limit_bytes=16 * 1024 * 1024)
@@ -125,7 +125,7 @@
             upg_s[there, :] = up_grad
         return carry
 
-    lax.fori_loop(0, rows_z, middle, 0, unroll=2)
+    lax.fori_loop(0, rows_z, middle, 0, unroll=4)
 
     def slots_of(left, right, outs, shift):
         rows = total // len(outs)
@@ -185,6 +185,28 @@
     out[:, SPLIT:] = high_low(value)
 
 
+def touch_kernel(*refs):
+    ins, out = refs[:-1], refs[-1]
+    total = ins[0][:8, :LANES].astype(jnp.float32)
+    for ref in ins[1:]:
+        total = total + ref[:8, :LANES].astype(jnp.float32)
+    out[...] = total
+
+
+def touch_call(weights):
+    return pl.pallas_call(
+        touch_kernel,
+        out_shape=jax.ShapeDtypeStruct((8, LANES), jnp.float32),
+        in_specs=[VMEM] * len(weights),
+        out_specs=VMEM,
+        compiler_params=pltpu.CompilerParams(
+            vmem_limit_bytes=8 * 1024 * 1024, has_side_effects=True
+        ),
+        cost_estimate=cost(1 << 10),
+        name="touch_weights",
+    )(*weights)
+
+
 def sum_a_kernel(slots, *refs):
     outs = refs[-(refs[0].shape[0] // slots) :]
     ins = refs[: len(refs) - len(outs)]
@@ -280,6 +302,7 @@
         rows_y * slots, model_width
     )
     tokens_z = jnp.concatenate(ring(owned, Z, split=False), axis=0)
+    touch_call([w_gate[0], w_up[0], w_down[0]])
     token_blocks = ring(tokens_z, Y)
     scaled_blocks = ring(scaled_y, Z)
     (gathered, scaled, hidden, gate_pre_grad, up_pre_grad), out_a, out_b = main_call(

time: 196 us -> 192 us (0.980)
  waiting for transfers between devices: 63.3 us -> 57.7 us
    ppermute x36, waiting for transfers between devices: 55.7 us -> 50.1 us  [pass_on(): lax.ppermute(value, axis, [((i + back) % peers, i) for i in range(peers)])]
  transfers between devices with their start and end apart: 40 -> 40, of which waited for: 11 -> 12; matrix products, arithmetic and copies ran while one was open for 6% -> 10% of each run, Pallas kernels for 1% -> 1%
where the time goes in v2:
time: 192 us; the launch traced here: 191 us
  starting transfers between devices  95.8 us (50%)
  waiting for transfers between devices  57.7 us (30%)
  Pallas kernels  12.6 us (7%)
  local copies, waits for them, and re-layouts  12 us (6%)
  matrix products  11 us (6%)
    ppermute x36, starting transfers between devices, pass_on(): lax.ppermute(value, axis, [((i + back) % peers, i) for i in range(peers)])  67 us
    ppermute x36, waiting for transfers between devices, pass_on(): lax.ppermute(value, axis, [((i + back) % peers, i) for i in range(peers)])  50.1 us
    all_to_all x1, starting transfers between devices, on_device(): lax.all_to_all(tiles_b.reshape(rows_y * owners, capacity, narrow), (Y, 'e...  11 us
    pallas_call x1, Pallas kernels, main_call(): pl.pallas_call(functools.partial(main_kernel, rows_y, rows_z, slots, len(...  10.2 us
    unnamed x20, local copies, waits for them, and re-layouts  7.84 us
    all_to_all x1, starting transfers between devices, on_device(): lax.all_to_all(send_tokens.astype(bf).reshape(owners, capacity, model_wid...  6.47 us
    all_to_all x1, starting transfers between devices, on_device(): lax.all_to_all(slot_home.reshape(owners, capacity, wide), 'expert', 0, 0,...  5.92 us
    all_to_all x1, starting transfers between devices, on_device(): lax.all_to_all(copies, (Y, 'expert'), 0, 0, tiled=True)  5.38 us
  transfers between devices with their start and end apart: 40, of which 12 were waited for; matrix products, arithmetic and copies ran while one was open for 10% of the time, Pallas kernels for 1%

profile of v2, /device:TPU:1, one launch (start us, length us, event | category | flops | bytes accessed | tf_op | source)
XLA Modules:
  0.0 191.1 jit_solution(10143023879388043873)
XLA Ops:
  3.7 6.5 %all-to-all-start = ((bf16[8,2,4096]{2,1,0:T(2,128)(2,1)}), bf16[8,2,4096]{2,1,0:T(2,128)(2,1)S(1)}, u32[]{:S(2)}, u32[]{:S(2)}) async-start(bf16[8,2,4096]{2,1,0:T(2,128)(2,1)} %reshape.64), calls=%async_computation | async-start | bytes 262144 | tf_op jit(solution)/shard_map/all_to_all | solution.py:289
  12.6 2.8 %all-to-all-done = bf16[8,2,4096]{2,1,0:T(2,128)(2,1)S(1)} async-done(((bf16[8,2,4096]{2,1,0:T(2,128)(2,1)}), bf16[8,2,4096]{2,1,0:T(2,128)(2,1)S(1)}, u32[]{:S(2)}, u32[]{:S(2)}) %all-to-all-start) | async-done | bytes 131104 | tf_op jit(solution)/shard_map/all_to_all | solution.py:289
  15.4 5.4 %all-to-all-start.1 = ((bf16[32,2,4096]{2,1,0:T(2,128)(2,1)}), bf16[32,2,4096]{2,1,0:T(2,128)(2,1)S(1)}, u32[]{:S(2)}, u32[]{:S(2)}) async-start(bf16[32,2,4096]{2,1,0:T(2,128)(2,1)} %bitcast.3), calls=%async_computation.1 | async-start | bytes 1048576 | tf_op jit(solution)/shard_map/all_to_all | solution.py:301
  22.6 4.0 %collective-permute-start = (bf16[16,4096]{1,0:T(8,128)(2,1)S(1)}, bf16[16,4096]{1,0:T(8,128)(2,1)S(1)}, u32[]{:S(2)}, u32[]{:S(2)}) collective-permute-start(bf16[16,4096]{1,0:T(8,128)(2,1)S(1)} %reshape.65), channel_id=1, source_target_pairs={{1,0},{2,1},{3,2},{4,3},{5,4},{6,5},{7,6},{0,7},{9,8},{10,9},{11,1... | collective-permute-start | bytes 393224 | tf_op jit(solution)/shard_map/ppermute | solution.py:30
  27.3 2.9 %collective-permute-done.4 = bf16[16,4096]{1,0:T(8,128)(2,1)S(1)} collective-permute-done((bf16[16,4096]{1,0:T(8,128)(2,1)S(1)}, bf16[16,4096]{1,0:T(8,128)(2,1)S(1)}, u32[]{:S(2)}, u32[]{:S(2)}) %collective-permute-start.4) | collective-permute-done | bytes 131104 | tf_op jit(solution)/shard_map/ppermute | solution.py:30
  45.0 8.9 %collective-permute-done.3 = bf16[16,4096]{1,0:T(8,128)(2,1)S(1)} collective-permute-done((bf16[16,4096]{1,0:T(8,128)(2,1)}, bf16[16,4096]{1,0:T(8,128)(2,1)S(1)}, u32[]{:S(2)}, u32[]{:S(2)}) %collective-permute-start.3) | collective-permute-done | bytes 131104 | tf_op jit(solution)/shard_map/ppermute | solution.py:30
  59.3 3.4 %collective-permute-start.12 = (bf16[64,4096]{1,0:T(8,128)(2,1)S(1)}, bf16[64,4096]{1,0:T(8,128)(2,1)S(1)}, u32[]{:S(2)}, u32[]{:S(2)}) collective-permute-start(bf16[64,4096]{1,0:T(8,128)(2,1)S(1)} %collective-permute-done.11.refs_6_), channel_id=1, source_target_pairs={{1,0},{2,1},{3,2},{4,3},{5,4},{6,5},{7,6},{0,7},{9,8},{10,9},{11,1... | collective-permute-start | bytes 1572872 | tf_op jit(solution)/shard_map/ppermute | solution.py:30
  62.7 8.5 %collective-permute-done.16.refs_12_ = bf16[64,4096]{1,0:T(8,128)(2,1)S(1)} collective-permute-done((bf16[64,4096]{1,0:T(8,128)(2,1)S(1)}, bf16[64,4096]{1,0:T(8,128)(2,1)S(1)}, u32[]{:S(2)}, u32[]{:S(2)}) %collective-permute-start.16) | collective-permute-done | bytes 524320 | tf_op jit(solution)/shard_map/ppermute | solution.py:30
  73.8 5.7 %collective-permute-done.9.refs_4_ = bf16[128,4096]{1,0:T(8,128)(2,1)S(1)} collective-permute-done((bf16[128,4096]{1,0:T(8,128)(2,1)}, bf16[128,4096]{1,0:T(8,128)(2,1)S(1)}, u32[]{:S(2)}, u32[]{:S(2)}) %collective-permute-start.9) | collective-permute-done | bytes 1048608 | tf_op jit(solution)/shard_map/ppermute | solution.py:30
  79.7 2.7 %collective-permute-start.8 = (bf16[64,4096]{1,0:T(8,128)(2,1)S(1)}, bf16[64,4096]{1,0:T(8,128)(2,1)S(1)}, u32[]{:S(2)}, u32[]{:S(2)}) collective-permute-start(bf16[64,4096]{1,0:T(8,128)(2,1)S(1)} %slice.24), channel_id=1, source_target_pairs={{8,0},{16,8},{24,16},{0,24},{9,1},{17,9},{25,17},{1,25},{10,2},{18... | collective-permute-start | bytes 1572872 | tf_op jit(solution)/shard_map/ppermute | solution.py:30
  82.6 3.4 %collective-permute-start.14 = (bf16[32,4096]{1,0:T(8,128)(2,1)S(1)}, bf16[32,4096]{1,0:T(8,128)(2,1)S(1)}, u32[]{:S(2)}, u32[]{:S(2)}) collective-permute-start(bf16[32,4096]{1,0:T(8,128)(2,1)S(1)} %slice.26), channel_id=1, source_target_pairs={{1,0},{2,1},{3,2},{4,3},{5,4},{6,5},{7,6},{0,7},{9,8},{10,9},{11,1... | collective-permute-start | bytes 786440 | tf_op jit(solution)/shard_map/ppermute | solution.py:30
  86.0 4.3 %collective-permute-done.10.refs_3_ = bf16[64,4096]{1,0:T(8,128)(2,1)S(1)} collective-permute-done((bf16[64,4096]{1,0:T(8,128)(2,1)S(1)}, bf16[64,4096]{1,0:T(8,128)(2,1)S(1)}, u32[]{:S(2)}, u32[]{:S(2)}) %collective-permute-start.10) | collective-permute-done | bytes 524320 | tf_op jit(solution)/shard_map/ppermute | solution.py:30
  90.3 10.2 %experts.1 = (bf16[512,4096]{1,0:T(8,128)(2,1)S(1)}, bf16[512,4096]{1,0:T(8,128)(2,1)S(1)}, bf16[512,224]{1,0:T(8,128)(2,1)S(1)}, bf16[512,224]{1,0:T(8,128)(2,1...) custom-call(s32[1]{0:T(128)} %bitcast.4.place, ...), custom_call_target="tpu_custom_call" | custom-call | flops 4697620480 | bytes 31457280 | tf_op jit(solution)/shard_map/experts/pallas_call | solution.py:162
  101.1 3.3 %collective-permute-start.20 = (bf16[128,2688]{1,0:T(8,128)(2,1)S(1)}, bf16[128,2688]{1,0:T(8,128)(2,1)S(1)}, u32[]{:S(2)}, u32[]{:S(2)}) collective-permute-start(bf16[128,2688]{1,0:T(8,128)(2,1)S(1)} %get-tuple-element.36), channel_id=1, source_target_pairs={{16,0},{24,8},{0,16},{8,24},{17,1},{25,9},{1,17},{9,25},{18,2},{26... | collective-permute-start | bytes 2064392 | tf_op jit(solution)/shard_map/ppermute | solution.py:30
  105.0 4.0 %collective-permute-start.29 = (bf16[64,1536]{1,0:T(8,128)(2,1)S(1)}, bf16[64,1536]{1,0:T(8,128)(2,1)S(1)}, u32[]{:S(2)}, u32[]{:S(2)}) collective-permute-start(bf16[64,1536]{1,0:T(8,128)(2,1)S(1)} %get-tuple-element.47), channel_id=1, source_target_pairs={{4,0},{5,1},{6,2},{7,3},{0,4},{1,5},{2,6},{3,7},{12,8},{13,9},{14,... | collective-permute-start | bytes 589832 | tf_op jit(solution)/shard_map/ppermute | solution.py:30
  114.0 4.0 %collective-permute-start.31 = (bf16[64,1536]{1,0:T(8,128)(2,1)S(1)}, bf16[64,1536]{1,0:T(8,128)(2,1)S(1)}, u32[]{:S(2)}, u32[]{:S(2)}) collective-permute-start(bf16[64,1536]{1,0:T(8,128)(2,1)S(1)} %get-tuple-element.49), channel_id=1, source_target_pairs={{3,0},{4,1},{5,2},{6,3},{7,4},{0,5},{1,6},{2,7},{11,8},{12,9},{13,... | collective-permute-start | bytes 589832 | tf_op jit(solution)/shard_map/ppermute | solution.py:30
  117.9 11.5 %collective-permute-done.20.refs_2_ = bf16[128,2688]{1,0:T(8,128)(2,1)S(1)} collective-permute-done((bf16[128,2688]{1,0:T(8,128)(2,1)S(1)}, bf16[128,2688]{1,0:T(8,128)(2,1)S(1)}, u32[]{:S(2)}, u32[]{:S(2)}) %collective-permute-start.20) | collective-permute-done | bytes 688160 | tf_op jit(solution)/shard_map/ppermute | solution.py:30
  139.5 3.9 %collective-permute-start.22 = (bf16[16,2688]{1,0:T(8,128)(2,1)S(1)}, bf16[16,2688]{1,0:T(8,128)(2,1)S(1)}, u32[]{:S(2)}, u32[]{:S(2)}) collective-permute-start(bf16[16,2688]{1,0:T(8,128)(2,1)S(1)} %get-tuple-element.39), channel_id=1, source_target_pairs={{4,0},{5,1},{6,2},{7,3},{0,4},{1,5},{2,6},{3,7},{12,8},{13,9},{14,... | collective-permute-start | bytes 258056 | tf_op jit(solution)/shard_map/ppermute | solution.py:30
  150.2 11.0 %all-to-all-start.3 = ((bf16[32,2,1536]{2,1,0:T(2,128)(2,1)}), bf16[32,2,1536]{2,1,0:T(2,128)(2,1)S(1)}, u32[]{:S(2)}, u32[]{:S(2)}) async-start(bf16[32,2,1536]{2,1,0:T(2,128)(2,1)} %bitcast.5), calls=%async_computation.3 | async-start | bytes 393216 | tf_op jit(solution)/shard_map/all_to_all | solution.py:333
  161.2 3.2 %collective-permute-start.24 = (bf16[16,2688]{1,0:T(8,128)(2,1)S(1)}, bf16[16,2688]{1,0:T(8,128)(2,1)S(1)}, u32[]{:S(2)}, u32[]{:S(2)}) collective-permute-start(bf16[16,2688]{1,0:T(8,128)(2,1)S(1)} %get-tuple-element.41), channel_id=1, source_target_pairs={{3,0},{4,1},{5,2},{6,3},{7,4},{0,5},{1,6},{2,7},{11,8},{12,9},{13,... | collective-permute-start | bytes 258056 | tf_op jit(solution)/shard_map/ppermute | solution.py:30
  164.7 5.6 %collective-permute-start.26 = (bf16[16,2688]{1,0:T(8,128)(2,1)S(1)}, bf16[16,2688]{1,0:T(8,128)(2,1)S(1)}, u32[]{:S(2)}, u32[]{:S(2)}) collective-permute-start(bf16[16,2688]{1,0:T(8,128)(2,1)S(1)} %get-tuple-element.43), channel_id=1, source_target_pairs={{2,0},{3,1},{4,2},{5,3},{6,4},{7,5},{0,6},{1,7},{10,8},{11,9},{12,... | collective-permute-start | bytes 258056 | tf_op jit(solution)/shard_map/ppermute | solution.py:30
  173.0 4.6 %fusion.2 = bf16[1,224,4096]{2,1,0:T(8,128)(2,1)} fusion(bf16[512,224]{1,0:T(8,128)(2,1)S(1)} %get-tuple-element.57, bf16[512,4096]{1,0:T(8,128)(2,1)} %copy-done.1), kind=kOutput, calls=%fused_computation.5 | convolution fusion | flops 940441600 | bytes 6258688 | tf_op jit(solution)/shard_map/dot_general | solution.py:313
  178.5 5.9 %all-to-all-start.2 = ((bf16[8,2,2688]{2,1,0:T(2,128)(2,1)}), bf16[8,2,2688]{2,1,0:T(2,128)(2,1)S(1)}, u32[]{:S(2)}, u32[]{:S(2)}) async-start(bf16[8,2,2688]{2,1,0:T(2,128)(2,1)} %reshape.67), calls=%async_computation.2 | async-start | bytes 172032 | tf_op jit(solution)/shard_map/all_to_all | solution.py:355
  184.7 4.7 %all-to-all-done.2 = bf16[8,2,2688]{2,1,0:T(2,128)(2,1)S(1)} async-done(((bf16[8,2,2688]{2,1,0:T(2,128)(2,1)}), bf16[8,2,2688]{2,1,0:T(2,128)(2,1)S(1)}, u32[]{:S(2)}, u32[]{:S(2)}) %all-to-all-start.2) | async-done | bytes 86048 | tf_op jit(solution)/shard_map/all_to_all | solution.py:355
  (110 shorter events, 59.9 us)
Async XLA Ops:
  3.7 11.7 %all-to-all-start = ((bf16[8,2,4096]{2,1,0:T(2,128)(2,1)}), bf16[8,2,4096]{2,1,0:T(2,128)(2,1)S(1)}, u32[]{:S(2)}, u32[]{:S(2)}) async-start(bf16[8,2,4096]{2,1,0:T(2,128)(2,1)} %reshape.64), calls=%async_computation | async-start | bytes 262144 | tf_op jit(solution)/shard_map/all_to_all | solution.py:289
  15.4 23.6 %all-to-all-start.1 = ((bf16[32,2,4096]{2,1,0:T(2,128)(2,1)}), bf16[32,2,4096]{2,1,0:T(2,128)(2,1)S(1)}, u32[]{:S(2)}, u32[]{:S(2)}) async-start(bf16[32,2,4096]{2,1,0:T(2,128)(2,1)} %bitcast.3), calls=%async_computation.1 | async-start | bytes 1048576 | tf_op jit(solution)/shard_map/all_to_all | solution.py:301
  35.6 19.0 %collective-permute-start.6 = (bf16[16,4096]{1,0:T(8,128)(2,1)S(1)}, bf16[16,4096]{1,0:T(8,128)(2,1)S(1)}, u32[]{:S(2)}, u32[]{:S(2)}) collective-permute-start(bf16[16,4096]{1,0:T(8,128)(2,1)S(1)} %collective-permute-done.5), channel_id=1, source_target_pairs={{7,0},{0,1},{1,2},{2,3},{3,4},{4,5},{5,6},{6,7},{15,8},{8,9},{9,10... | collective-permute-start | bytes 393224 | tf_op jit(solution)/shard_map/ppermute | solution.py:30
  39.2 20.1 %collective-permute-start.15 = (bf16[64,4096]{1,0:T(8,128)(2,1)S(1)}, bf16[64,4096]{1,0:T(8,128)(2,1)S(1)}, u32[]{:S(2)}, u32[]{:S(2)}) collective-permute-start(bf16[64,4096]{1,0:T(8,128)(2,1)S(1)} %reshape.66.refs_5_), channel_id=1, source_target_pairs={{7,0},{0,1},{1,2},{2,3},{3,4},{4,5},{5,6},{6,7},{15,8},{8,9},{9,10... | collective-permute-start | bytes 1572872 | tf_op jit(solution)/shard_map/ppermute | solution.py:30
  39.3 20.0 %collective-permute-start.11 = (bf16[64,4096]{1,0:T(8,128)(2,1)S(1)}, bf16[64,4096]{1,0:T(8,128)(2,1)S(1)}, u32[]{:S(2)}, u32[]{:S(2)}) collective-permute-start(bf16[64,4096]{1,0:T(8,128)(2,1)S(1)} %reshape.66.refs_5_), channel_id=1, source_target_pairs={{1,0},{2,1},{3,2},{4,3},{5,4},{6,5},{7,6},{0,7},{9,8},{10,9},{11,1... | collective-permute-start | bytes 1572872 | tf_op jit(solution)/shard_map/ppermute | solution.py:30
  41.9 12.0 %collective-permute-start.3 = (bf16[16,4096]{1,0:T(8,128)(2,1)}, bf16[16,4096]{1,0:T(8,128)(2,1)S(1)}, u32[]{:S(2)}, u32[]{:S(2)}) collective-permute-start(bf16[16,4096]{1,0:T(8,128)(2,1)} %collective-permute-done.2), channel_id=1, source_target_pairs={{1,0},{2,1},{3,2},{4,3},{5,4},{6,5},{7,6},{0,7},{9,8},{10,9},{11,1... | collective-permute-start | bytes 393224 | tf_op jit(solution)/shard_map/ppermute | solution.py:30
  56.6 22.9 %collective-permute-start.9 = (bf16[128,4096]{1,0:T(8,128)(2,1)}, bf16[128,4096]{1,0:T(8,128)(2,1)S(1)}, u32[]{:S(2)}, u32[]{:S(2)}) collective-permute-start(bf16[128,4096]{1,0:T(8,128)(2,1)} %constant_dynamic-update-slice_fusion.refs_0_), channel_id=1, source_target_pairs={{24,0},{0,8},{8,16},{16,24},{25,1},{1,9},{9,17},{17,25},{26,2},{2,... | collective-permute-start | bytes 3145736 | tf_op jit(solution)/shard_map/ppermute | solution.py:30
  57.8 21.8 %collective-permute-start.7 = (bf16[128,4096]{1,0:T(8,128)(2,1)}, bf16[128,4096]{1,0:T(8,128)(2,1)S(1)}, u32[]{:S(2)}, u32[]{:S(2)}) collective-permute-start(bf16[128,4096]{1,0:T(8,128)(2,1)} %constant_dynamic-update-slice_fusion.refs_0_), channel_id=1, source_target_pairs={{8,0},{16,8},{24,16},{0,24},{9,1},{17,9},{25,17},{1,25},{10,2},{18... | collective-permute-start | bytes 3145736 | tf_op jit(solution)/shard_map/ppermute | solution.py:30
  59.3 11.8 %collective-permute-start.16 = (bf16[64,4096]{1,0:T(8,128)(2,1)S(1)}, bf16[64,4096]{1,0:T(8,128)(2,1)S(1)}, u32[]{:S(2)}, u32[]{:S(2)}) collective-permute-start(bf16[64,4096]{1,0:T(8,128)(2,1)S(1)} %collective-permute-done.15.refs_13_), channel_id=1, source_target_pairs={{7,0},{0,1},{1,2},{2,3},{3,4},{4,5},{5,6},{6,7},{15,8},{8,9},{9,10... | collective-permute-start | bytes 1572872 | tf_op jit(solution)/shard_map/ppermute | solution.py:30
  59.3 11.8 %collective-permute-start.12 = (bf16[64,4096]{1,0:T(8,128)(2,1)S(1)}, bf16[64,4096]{1,0:T(8,128)(2,1)S(1)}, u32[]{:S(2)}, u32[]{:S(2)}) collective-permute-start(bf16[64,4096]{1,0:T(8,128)(2,1)S(1)} %collective-permute-done.11.refs_6_), channel_id=1, source_target_pairs={{1,0},{2,1},{3,2},{4,3},{5,4},{6,5},{7,6},{0,7},{9,8},{10,9},{11,1... | collective-permute-start | bytes 1572872 | tf_op jit(solution)/shard_map/ppermute | solution.py:30
  100.6 13.4 %collective-permute-start.19 = (bf16[128,2688]{1,0:T(8,128)(2,1)S(1)}, bf16[128,2688]{1,0:T(8,128)(2,1)S(1)}, u32[]{:S(2)}, u32[]{:S(2)}) collective-permute-start(bf16[128,2688]{1,0:T(8,128)(2,1)S(1)} %get-tuple-element.35), channel_id=1, source_target_pairs={{24,0},{0,8},{8,16},{16,24},{25,1},{1,9},{9,17},{17,25},{26,2},{2,... | collective-permute-start | bytes 2064392 | tf_op jit(solution)/shard_map/ppermute | solution.py:30
  101.1 28.3 %collective-permute-start.20 = (bf16[128,2688]{1,0:T(8,128)(2,1)S(1)}, bf16[128,2688]{1,0:T(8,128)(2,1)S(1)}, u32[]{:S(2)}, u32[]{:S(2)}) collective-permute-start(bf16[128,2688]{1,0:T(8,128)(2,1)S(1)} %get-tuple-element.36), channel_id=1, source_target_pairs={{16,0},{24,8},{0,16},{8,24},{17,1},{25,9},{1,17},{9,25},{18,2},{26... | collective-permute-start | bytes 2064392 | tf_op jit(solution)/shard_map/ppermute | solution.py:30
  104.4 29.6 %collective-permute-start.21 = (bf16[128,2688]{1,0:T(8,128)(2,1)S(1)}, bf16[128,2688]{1,0:T(8,128)(2,1)S(1)}, u32[]{:S(2)}, u32[]{:S(2)}) collective-permute-start(bf16[128,2688]{1,0:T(8,128)(2,1)S(1)} %get-tuple-element.37), channel_id=1, source_target_pairs={{8,0},{16,8},{24,16},{0,24},{9,1},{17,9},{25,17},{1,25},{10,2},{18... | collective-permute-start | bytes 2064392 | tf_op jit(solution)/shard_map/ppermute | solution.py:30
  105.0 31.5 %collective-permute-start.29 = (bf16[64,1536]{1,0:T(8,128)(2,1)S(1)}, bf16[64,1536]{1,0:T(8,128)(2,1)S(1)}, u32[]{:S(2)}, u32[]{:S(2)}) collective-permute-start(bf16[64,1536]{1,0:T(8,128)(2,1)S(1)} %get-tuple-element.47), channel_id=1, source_target_pairs={{4,0},{5,1},{6,2},{7,3},{0,4},{1,5},{2,6},{3,7},{12,8},{13,9},{14,... | collective-permute-start | bytes 589832 | tf_op jit(solution)/shard_map/ppermute | solution.py:30
  109.0 29.9 %collective-permute-start.30 = (bf16[64,1536]{1,0:T(8,128)(2,1)S(1)}, bf16[64,1536]{1,0:T(8,128)(2,1)S(1)}, u32[]{:S(2)}, u32[]{:S(2)}) collective-permute-start(bf16[64,1536]{1,0:T(8,128)(2,1)S(1)} %get-tuple-element.48), channel_id=1, source_target_pairs={{5,0},{6,1},{7,2},{0,3},{1,4},{2,5},{3,6},{4,7},{13,8},{14,9},{15,... | collective-permute-start | bytes 589832 | tf_op jit(solution)/shard_map/ppermute | solution.py:30
  114.0 25.5 %collective-permute-start.31 = (bf16[64,1536]{1,0:T(8,128)(2,1)S(1)}, bf16[64,1536]{1,0:T(8,128)(2,1)S(1)}, u32[]{:S(2)}, u32[]{:S(2)}) collective-permute-start(bf16[64,1536]{1,0:T(8,128)(2,1)S(1)} %get-tuple-element.49), channel_id=1, source_target_pairs={{3,0},{4,1},{5,2},{6,3},{7,4},{0,5},{1,6},{2,7},{11,8},{12,9},{13,... | collective-permute-start | bytes 589832 | tf_op jit(solution)/shard_map/ppermute | solution.py:30
  129.4 13.9 %collective-permute-start.32 = (bf16[64,1536]{1,0:T(8,128)(2,1)S(1)}, bf16[64,1536]{1,0:T(8,128)(2,1)S(1)}, u32[]{:S(2)}, u32[]{:S(2)}) collective-permute-start(bf16[64,1536]{1,0:T(8,128)(2,1)S(1)} %get-tuple-element.50), channel_id=1, source_target_pairs={{6,0},{7,1},{0,2},{1,3},{2,4},{3,5},{4,6},{5,7},{14,8},{15,9},{8,1... | collective-permute-start | bytes 589832 | tf_op jit(solution)/shard_map/ppermute | solution.py:30
  134.0 11.8 %collective-permute-start.33 = (bf16[64,1536]{1,0:T(8,128)(2,1)S(1)}, bf16[64,1536]{1,0:T(8,128)(2,1)S(1)}, u32[]{:S(2)}, u32[]{:S(2)}) collective-permute-start(bf16[64,1536]{1,0:T(8,128)(2,1)S(1)} %get-tuple-element.51), channel_id=1, source_target_pairs={{2,0},{3,1},{4,2},{5,3},{6,4},{7,5},{0,6},{1,7},{10,8},{11,9},{12,... | collective-permute-start | bytes 589832 | tf_op jit(solution)/shard_map/ppermute | solution.py:30
  139.5 30.8 %collective-permute-start.22 = (bf16[16,2688]{1,0:T(8,128)(2,1)S(1)}, bf16[16,2688]{1,0:T(8,128)(2,1)S(1)}, u32[]{:S(2)}, u32[]{:S(2)}) collective-permute-start(bf16[16,2688]{1,0:T(8,128)(2,1)S(1)} %get-tuple-element.39), channel_id=1, source_target_pairs={{4,0},{5,1},{6,2},{7,3},{0,4},{1,5},{2,6},{3,7},{12,8},{13,9},{14,... | collective-permute-start | bytes 258056 | tf_op jit(solution)/shard_map/ppermute | solution.py:30
  143.4 26.9 %collective-permute-start.23 = (bf16[16,2688]{1,0:T(8,128)(2,1)S(1)}, bf16[16,2688]{1,0:T(8,128)(2,1)S(1)}, u32[]{:S(2)}, u32[]{:S(2)}) collective-permute-start(bf16[16,2688]{1,0:T(8,128)(2,1)S(1)} %get-tuple-element.40), channel_id=1, source_target_pairs={{5,0},{6,1},{7,2},{0,3},{1,4},{2,5},{3,6},{4,7},{13,8},{14,9},{15,... | collective-permute-start | bytes 258056 | tf_op jit(solution)/shard_map/ppermute | solution.py:30
  150.2 27.3 %all-to-all-start.3 = ((bf16[32,2,1536]{2,1,0:T(2,128)(2,1)}), bf16[32,2,1536]{2,1,0:T(2,128)(2,1)S(1)}, u32[]{:S(2)}, u32[]{:S(2)}) async-start(bf16[32,2,1536]{2,1,0:T(2,128)(2,1)} %bitcast.5), calls=%async_computation.3 | async-start | bytes 393216 | tf_op jit(solution)/shard_map/all_to_all | solution.py:333
  161.2 16.4 %collective-permute-start.24 = (bf16[16,2688]{1,0:T(8,128)(2,1)S(1)}, bf16[16,2688]{1,0:T(8,128)(2,1)S(1)}, u32[]{:S(2)}, u32[]{:S(2)}) collective-permute-start(bf16[16,2688]{1,0:T(8,128)(2,1)S(1)} %get-tuple-element.41), channel_id=1, source_target_pairs={{3,0},{4,1},{5,2},{6,3},{7,4},{0,5},{1,6},{2,7},{11,8},{12,9},{13,... | collective-permute-start | bytes 258056 | tf_op jit(solution)/shard_map/ppermute | solution.py:30
  164.4 13.2 %collective-permute-start.25 = (bf16[16,2688]{1,0:T(8,128)(2,1)S(1)}, bf16[16,2688]{1,0:T(8,128)(2,1)S(1)}, u32[]{:S(2)}, u32[]{:S(2)}) collective-permute-start(bf16[16,2688]{1,0:T(8,128)(2,1)S(1)} %get-tuple-element.42), channel_id=1, source_target_pairs={{6,0},{7,1},{0,2},{1,3},{2,4},{3,5},{4,6},{5,7},{14,8},{15,9},{8,1... | collective-permute-start | bytes 258056 | tf_op jit(solution)/shard_map/ppermute | solution.py:30
  164.7 12.9 %collective-permute-start.26 = (bf16[16,2688]{1,0:T(8,128)(2,1)S(1)}, bf16[16,2688]{1,0:T(8,128)(2,1)S(1)}, u32[]{:S(2)}, u32[]{:S(2)}) collective-permute-start(bf16[16,2688]{1,0:T(8,128)(2,1)S(1)} %get-tuple-element.43), channel_id=1, source_target_pairs={{2,0},{3,1},{4,2},{5,3},{6,4},{7,5},{0,6},{1,7},{10,8},{11,9},{12,... | collective-permute-start | bytes 258056 | tf_op jit(solution)/shard_map/ppermute | solution.py:30
  (21 other events, 356.2 us)

commit v3 on v2

--- a/solution.py
+++ b/solution.py
@@ -81,11 +81,18 @@
 
     def forward(step, carry):
         cols = pl.ds(pl.multiple_of(step * CHUNK, CHUNK), CHUNK)
-        for blocks, whole in ((token_refs, t_all), (scaled_refs, s_all)):
-            row = 0
-            for block in blocks:
-                whole[row : row + block.shape[0], cols] = block[:, cols]
-                row += block.shape[0]
+        row = 0
+        for block in token_refs:
+            t_all[row : row + block.shape[0], cols] = block[:, cols]
+            row += block.shape[0]
+        tile = 0
+        for block in scaled_refs:
+            for k in range(block.shape[0] // slots):
+                dz, at_y = tile // rows_y, tile % rows_y
+                dy = lax.rem(at_y + rows_y - place[0], rows_y)
+                rows = pl.ds(pl.multiple_of((dz * rows_y + dy) * slots, slots), slots)
+                s_all[rows, cols] = block[k * slots : (k + 1) * slots, cols]
+                tile += 1
         rows_t = t_all[:, cols]
         acc_g[...] += lax.dot_general(
             rows_t, wg[:, cols], CONTRACT, preferred_element_type=jnp.float32
@@ -100,11 +107,10 @@
 
     lax.fori_loop(0, width // CHUNK, forward, 0)
 
-    def middle(dz, carry):
+    for dz in range(rows_z):
         for dy in range(rows_y):
-            here = pl.ds(pl.multiple_of((dy * rows_z + dz) * slots, slots), slots)
-            at_y = lax.rem(place[0] + dy, rows_y)
-            there = pl.ds(pl.multiple_of((dz * rows_y + at_y) * slots, slots), slots)
+            here = pl.ds((dy * rows_z + dz) * slots, slots)
+            there = pl.ds((dz * rows_y + dy) * slots, slots)
             gate_pre = acc_g[here, :]
             up_pre = acc_u[here, :]
             hidden_grad = acc_h[there, :]
@@ -123,9 +129,6 @@
             upg_t[here, :] = up_grad
             gpg_s[there, :] = gate_grad
             upg_s[there, :] = up_grad
-        return carry
-
-    lax.fori_loop(0, rows_z, middle, 0, unroll=4)
 
     def slots_of(left, right, outs, shift):
         rows = total // len(outs)
@@ -226,18 +229,19 @@
         add_narrow(ins, slice(k * slots, (k + 1) * slots), out)
 
 
-def sum_b_kernel(slots, *refs):
+def sum_b_kernel(slots, place, *refs):
     ins, out = refs[:-1], refs[-1]
     peers, owners, capacity = out.shape[0], out.shape[1], out.shape[2]
 
     def step(k, carry):
         rows = pl.ds(pl.multiple_of(k * slots, slots), slots)
+        target = lax.rem(place[0] + k, peers)
         total = ins[0][rows, :].astype(jnp.float32)
         for ref in ins[1:]:
             total = total + ref[rows, :].astype(jnp.float32)
         total = total.astype(jnp.bfloat16)
         for e in range(owners):
-            out[k, e] = total[e * capacity : (e + 1) * capacity]
+            out[target, e] = total[e * capacity : (e + 1) * capacity]
         return carry
 
     lax.fori_loop(0, peers, step, 0)
@@ -324,12 +328,12 @@
     tiles_b = pl.pallas_call(
         functools.partial(sum_b_kernel, slots),
         out_shape=jax.ShapeDtypeStruct((rows_y, owners, capacity, narrow), bf),
-        in_specs=[VMEM] * rows_z,
+        in_specs=[SMEM] + [VMEM] * rows_z,
         out_specs=VMEM,
         compiler_params=SMALL,
         cost_estimate=cost(rows_y * rows_z * slots * narrow),
         name="sum_z",
-    )(out_b[0], *arrived_b)
+    )(place, out_b[0], *arrived_b)
     back_b = lax.all_to_all(
         tiles_b.reshape(rows_y * owners, capacity, narrow), (Y, "expert"), 0, 0, tiled=True
     ).reshape(rows_y * slots, narrow)

time: 192 us -> 192 us (level)
  no operation moved by 1% of the time
where the time goes in v3:
time: 192 us; the launch traced here: 191 us
  starting transfers between devices  95.1 us (50%)
  waiting for transfers between devices  58.3 us (30%)
  Pallas kernels  12.5 us (7%)
  local copies, waits for them, and re-layouts  12 us (6%)
  matrix products  10.9 us (6%)
    ppermute x36, starting transfers between devices, pass_on(): lax.ppermute(value, axis, [((i + back) % peers, i) for i in range(peers)])  66.7 us
    ppermute x36, waiting for transfers between devices, pass_on(): lax.ppermute(value, axis, [((i + back) % peers, i) for i in range(peers)])  50.8 us
    all_to_all x1, starting transfers between devices, on_device(): lax.all_to_all(tiles_b.reshape(rows_y * owners, capacity, narrow), (Y, 'e...  10.6 us
    pallas_call x1, Pallas kernels, main_call(): pl.pallas_call(functools.partial(main_kernel, rows_y, rows_z, slots, len(...  10.2 us
    unnamed x20, local copies, waits for them, and re-layouts  7.84 us
    all_to_all x1, starting transfers between devices, on_device(): lax.all_to_all(send_tokens.astype(bf).reshape(owners, capacity, model_wid...  6.47 us
    all_to_all x1, starting transfers between devices, on_device(): lax.all_to_all(slot_home.reshape(owners, capacity, wide), 'expert', 0, 0,...  5.92 us
    all_to_all x1, starting transfers between devices, on_device(): lax.all_to_all(copies, (Y, 'expert'), 0, 0, tiled=True)  5.38 us
  transfers between devices with their start and end apart: 40, of which 12 were waited for; matrix products, arithmetic and copies ran while one was open for 10% of the time, Pallas kernels for 1%

profile of v3, /device:TPU:1, one launch (start us, length us, event | category | flops | bytes accessed | tf_op | source)
XLA Modules:
  0.0 191.0 jit_solution(893857806648056332)
XLA Ops:
  3.7 6.5 %all-to-all-start = ((bf16[8,2,4096]{2,1,0:T(2,128)(2,1)}), bf16[8,2,4096]{2,1,0:T(2,128)(2,1)S(1)}, u32[]{:S(2)}, u32[]{:S(2)}) async-start(bf16[8,2,4096]{2,1,0:T(2,128)(2,1)} %reshape.64), calls=%async_computation | async-start | bytes 262144 | tf_op jit(solution)/shard_map/all_to_all | solution.py:293
  12.6 2.8 %all-to-all-done = bf16[8,2,4096]{2,1,0:T(2,128)(2,1)S(1)} async-done(((bf16[8,2,4096]{2,1,0:T(2,128)(2,1)}), bf16[8,2,4096]{2,1,0:T(2,128)(2,1)S(1)}, u32[]{:S(2)}, u32[]{:S(2)}) %all-to-all-start) | async-done | bytes 131104 | tf_op jit(solution)/shard_map/all_to_all | solution.py:293
  15.4 5.4 %all-to-all-start.1 = ((bf16[32,2,4096]{2,1,0:T(2,128)(2,1)}), bf16[32,2,4096]{2,1,0:T(2,128)(2,1)S(1)}, u32[]{:S(2)}, u32[]{:S(2)}) async-start(bf16[32,2,4096]{2,1,0:T(2,128)(2,1)} %bitcast.3), calls=%async_computation.1 | async-start | bytes 1048576 | tf_op jit(solution)/shard_map/all_to_all | solution.py:305
  22.6 4.0 %collective-permute-start = (bf16[16,4096]{1,0:T(8,128)(2,1)S(1)}, bf16[16,4096]{1,0:T(8,128)(2,1)S(1)}, u32[]{:S(2)}, u32[]{:S(2)}) collective-permute-start(bf16[16,4096]{1,0:T(8,128)(2,1)S(1)} %reshape.65), channel_id=1, source_target_pairs={{1,0},{2,1},{3,2},{4,3},{5,4},{6,5},{7,6},{0,7},{9,8},{10,9},{11,1... | collective-permute-start | bytes 393224 | tf_op jit(solution)/shard_map/ppermute | solution.py:30
  27.3 2.9 %collective-permute-done.4 = bf16[16,4096]{1,0:T(8,128)(2,1)S(1)} collective-permute-done((bf16[16,4096]{1,0:T(8,128)(2,1)S(1)}, bf16[16,4096]{1,0:T(8,128)(2,1)S(1)}, u32[]{:S(2)}, u32[]{:S(2)}) %collective-permute-start.4) | collective-permute-done | bytes 131104 | tf_op jit(solution)/shard_map/ppermute | solution.py:30
  45.0 8.9 %collective-permute-done.3 = bf16[16,4096]{1,0:T(8,128)(2,1)S(1)} collective-permute-done((bf16[16,4096]{1,0:T(8,128)(2,1)}, bf16[16,4096]{1,0:T(8,128)(2,1)S(1)}, u32[]{:S(2)}, u32[]{:S(2)}) %collective-permute-start.3) | collective-permute-done | bytes 131104 | tf_op jit(solution)/shard_map/ppermute | solution.py:30
  59.3 3.4 %collective-permute-start.12 = (bf16[64,4096]{1,0:T(8,128)(2,1)S(1)}, bf16[64,4096]{1,0:T(8,128)(2,1)S(1)}, u32[]{:S(2)}, u32[]{:S(2)}) collective-permute-start(bf16[64,4096]{1,0:T(8,128)(2,1)S(1)} %collective-permute-done.11.refs_6_), channel_id=1, source_target_pairs={{1,0},{2,1},{3,2},{4,3},{5,4},{6,5},{7,6},{0,7},{9,8},{10,9},{11,1... | collective-permute-start | bytes 1572872 | tf_op jit(solution)/shard_map/ppermute | solution.py:30
  62.7 8.5 %collective-permute-done.16.refs_12_ = bf16[64,4096]{1,0:T(8,128)(2,1)S(1)} collective-permute-done((bf16[64,4096]{1,0:T(8,128)(2,1)S(1)}, bf16[64,4096]{1,0:T(8,128)(2,1)S(1)}, u32[]{:S(2)}, u32[]{:S(2)}) %collective-permute-start.16) | collective-permute-done | bytes 524320 | tf_op jit(solution)/shard_map/ppermute | solution.py:30
  73.8 5.7 %collective-permute-done.9.refs_4_ = bf16[128,4096]{1,0:T(8,128)(2,1)S(1)} collective-permute-done((bf16[128,4096]{1,0:T(8,128)(2,1)}, bf16[128,4096]{1,0:T(8,128)(2,1)S(1)}, u32[]{:S(2)}, u32[]{:S(2)}) %collective-permute-start.9) | collective-permute-done | bytes 1048608 | tf_op jit(solution)/shard_map/ppermute | solution.py:30
  79.7 2.7 %collective-permute-start.8 = (bf16[64,4096]{1,0:T(8,128)(2,1)S(1)}, bf16[64,4096]{1,0:T(8,128)(2,1)S(1)}, u32[]{:S(2)}, u32[]{:S(2)}) collective-permute-start(bf16[64,4096]{1,0:T(8,128)(2,1)S(1)} %slice.24), channel_id=1, source_target_pairs={{8,0},{16,8},{24,16},{0,24},{9,1},{17,9},{25,17},{1,25},{10,2},{18... | collective-permute-start | bytes 1572872 | tf_op jit(solution)/shard_map/ppermute | solution.py:30
  82.6 3.4 %collective-permute-start.14 = (bf16[32,4096]{1,0:T(8,128)(2,1)S(1)}, bf16[32,4096]{1,0:T(8,128)(2,1)S(1)}, u32[]{:S(2)}, u32[]{:S(2)}) collective-permute-start(bf16[32,4096]{1,0:T(8,128)(2,1)S(1)} %slice.26), channel_id=1, source_target_pairs={{1,0},{2,1},{3,2},{4,3},{5,4},{6,5},{7,6},{0,7},{9,8},{10,9},{11,1... | collective-permute-start | bytes 786440 | tf_op jit(solution)/shard_map/ppermute | solution.py:30
  86.0 4.3 %collective-permute-done.10.refs_3_ = bf16[64,4096]{1,0:T(8,128)(2,1)S(1)} collective-permute-done((bf16[64,4096]{1,0:T(8,128)(2,1)S(1)}, bf16[64,4096]{1,0:T(8,128)(2,1)S(1)}, u32[]{:S(2)}, u32[]{:S(2)}) %collective-permute-start.10) | collective-permute-done | bytes 524320 | tf_op jit(solution)/shard_map/ppermute | solution.py:30
  90.3 10.2 %experts.1 = (bf16[512,4096]{1,0:T(8,128)(2,1)S(1)}, bf16[512,4096]{1,0:T(8,128)(2,1)S(1)}, bf16[512,224]{1,0:T(8,128)(2,1)S(1)}, bf16[512,224]{1,0:T(8,128)(2,1...) custom-call(s32[1]{0:T(128)} %bitcast.4.place, ...), custom_call_target="tpu_custom_call" | custom-call | flops 4697620480 | bytes 31457280 | tf_op jit(solution)/shard_map/experts/pallas_call | solution.py:165
  101.0 3.3 %collective-permute-start.20 = (bf16[128,2688]{1,0:T(8,128)(2,1)S(1)}, bf16[128,2688]{1,0:T(8,128)(2,1)S(1)}, u32[]{:S(2)}, u32[]{:S(2)}) collective-permute-start(bf16[128,2688]{1,0:T(8,128)(2,1)S(1)} %get-tuple-element.36), channel_id=1, source_target_pairs={{16,0},{24,8},{0,16},{8,24},{17,1},{25,9},{1,17},{9,25},{18,2},{26... | collective-permute-start | bytes 2064392 | tf_op jit(solution)/shard_map/ppermute | solution.py:30
  105.0 4.0 %collective-permute-start.29 = (bf16[64,1536]{1,0:T(8,128)(2,1)S(1)}, bf16[64,1536]{1,0:T(8,128)(2,1)S(1)}, u32[]{:S(2)}, u32[]{:S(2)}) collective-permute-start(bf16[64,1536]{1,0:T(8,128)(2,1)S(1)} %get-tuple-element.47), channel_id=1, source_target_pairs={{4,0},{5,1},{6,2},{7,3},{0,4},{1,5},{2,6},{3,7},{12,8},{13,9},{14,... | collective-permute-start | bytes 589832 | tf_op jit(solution)/shard_map/ppermute | solution.py:30
  113.9 3.9 %collective-permute-start.31 = (bf16[64,1536]{1,0:T(8,128)(2,1)S(1)}, bf16[64,1536]{1,0:T(8,128)(2,1)S(1)}, u32[]{:S(2)}, u32[]{:S(2)}) collective-permute-start(bf16[64,1536]{1,0:T(8,128)(2,1)S(1)} %get-tuple-element.49), channel_id=1, source_target_pairs={{3,0},{4,1},{5,2},{6,3},{7,4},{0,5},{1,6},{2,7},{11,8},{12,9},{13,... | collective-permute-start | bytes 589832 | tf_op jit(solution)/shard_map/ppermute | solution.py:30
  117.9 11.5 %collective-permute-done.20.refs_2_ = bf16[128,2688]{1,0:T(8,128)(2,1)S(1)} collective-permute-done((bf16[128,2688]{1,0:T(8,128)(2,1)S(1)}, bf16[128,2688]{1,0:T(8,128)(2,1)S(1)}, u32[]{:S(2)}, u32[]{:S(2)}) %collective-permute-start.20) | collective-permute-done | bytes 688160 | tf_op jit(solution)/shard_map/ppermute | solution.py:30
  139.2 3.9 %collective-permute-start.22 = (bf16[16,2688]{1,0:T(8,128)(2,1)S(1)}, bf16[16,2688]{1,0:T(8,128)(2,1)S(1)}, u32[]{:S(2)}, u32[]{:S(2)}) collective-permute-start(bf16[16,2688]{1,0:T(8,128)(2,1)S(1)} %get-tuple-element.39), channel_id=1, source_target_pairs={{4,0},{5,1},{6,2},{7,3},{0,4},{1,5},{2,6},{3,7},{12,8},{13,9},{14,... | collective-permute-start | bytes 258056 | tf_op jit(solution)/shard_map/ppermute | solution.py:30
  150.6 10.6 %all-to-all-start.3 = ((bf16[32,2,1536]{2,1,0:T(2,128)(2,1)}), bf16[32,2,1536]{2,1,0:T(2,128)(2,1)S(1)}, u32[]{:S(2)}, u32[]{:S(2)}) async-start(bf16[32,2,1536]{2,1,0:T(2,128)(2,1)} %bitcast.5), calls=%async_computation.3 | async-start | bytes 393216 | tf_op jit(solution)/shard_map/all_to_all | solution.py:337
  161.2 3.0 %collective-permute-start.24 = (bf16[16,2688]{1,0:T(8,128)(2,1)S(1)}, bf16[16,2688]{1,0:T(8,128)(2,1)S(1)}, u32[]{:S(2)}, u32[]{:S(2)}) collective-permute-start(bf16[16,2688]{1,0:T(8,128)(2,1)S(1)} %get-tuple-element.41), channel_id=1, source_target_pairs={{3,0},{4,1},{5,2},{6,3},{7,4},{0,5},{1,6},{2,7},{11,8},{12,9},{13,... | collective-permute-start | bytes 258056 | tf_op jit(solution)/shard_map/ppermute | solution.py:30
  164.7 5.5 %collective-permute-start.26 = (bf16[16,2688]{1,0:T(8,128)(2,1)S(1)}, bf16[16,2688]{1,0:T(8,128)(2,1)S(1)}, u32[]{:S(2)}, u32[]{:S(2)}) collective-permute-start(bf16[16,2688]{1,0:T(8,128)(2,1)S(1)} %get-tuple-element.43), channel_id=1, source_target_pairs={{2,0},{3,1},{4,2},{5,3},{6,4},{7,5},{0,6},{1,7},{10,8},{11,9},{12,... | collective-permute-start | bytes 258056 | tf_op jit(solution)/shard_map/ppermute | solution.py:30
  172.9 4.6 %fusion.2 = bf16[1,224,4096]{2,1,0:T(8,128)(2,1)} fusion(bf16[512,224]{1,0:T(8,128)(2,1)S(1)} %get-tuple-element.57, bf16[512,4096]{1,0:T(8,128)(2,1)} %copy-done.1), kind=kOutput, calls=%fused_computation.5 | convolution fusion | flops 940441600 | bytes 6258688 | tf_op jit(solution)/shard_map/dot_general | solution.py:317
  178.4 5.9 %all-to-all-start.2 = ((bf16[8,2,2688]{2,1,0:T(2,128)(2,1)}), bf16[8,2,2688]{2,1,0:T(2,128)(2,1)S(1)}, u32[]{:S(2)}, u32[]{:S(2)}) async-start(bf16[8,2,2688]{2,1,0:T(2,128)(2,1)} %reshape.67), calls=%async_computation.2 | async-start | bytes 172032 | tf_op jit(solution)/shard_map/all_to_all | solution.py:359
  184.6 4.7 %all-to-all-done.2 = bf16[8,2,2688]{2,1,0:T(2,128)(2,1)S(1)} async-done(((bf16[8,2,2688]{2,1,0:T(2,128)(2,1)}), bf16[8,2,2688]{2,1,0:T(2,128)(2,1)S(1)}, u32[]{:S(2)}, u32[]{:S(2)}) %all-to-all-start.2) | async-done | bytes 86048 | tf_op jit(solution)/shard_map/all_to_all | solution.py:359
  (110 shorter events, 60.5 us)
Async XLA Ops:
  3.7 11.7 %all-to-all-start = ((bf16[8,2,4096]{2,1,0:T(2,128)(2,1)}), bf16[8,2,4096]{2,1,0:T(2,128)(2,1)S(1)}, u32[]{:S(2)}, u32[]{:S(2)}) async-start(bf16[8,2,4096]{2,1,0:T(2,128)(2,1)} %reshape.64), calls=%async_computation | async-start | bytes 262144 | tf_op jit(solution)/shard_map/all_to_all | solution.py:293
  15.4 23.5 %all-to-all-start.1 = ((bf16[32,2,4096]{2,1,0:T(2,128)(2,1)}), bf16[32,2,4096]{2,1,0:T(2,128)(2,1)S(1)}, u32[]{:S(2)}, u32[]{:S(2)}) async-start(bf16[32,2,4096]{2,1,0:T(2,128)(2,1)} %bitcast.3), calls=%async_computation.1 | async-start | bytes 1048576 | tf_op jit(solution)/shard_map/all_to_all | solution.py:305
  35.6 19.0 %collective-permute-start.6 = (bf16[16,4096]{1,0:T(8,128)(2,1)S(1)}, bf16[16,4096]{1,0:T(8,128)(2,1)S(1)}, u32[]{:S(2)}, u32[]{:S(2)}) collective-permute-start(bf16[16,4096]{1,0:T(8,128)(2,1)S(1)} %collective-permute-done.5), channel_id=1, source_target_pairs={{7,0},{0,1},{1,2},{2,3},{3,4},{4,5},{5,6},{6,7},{15,8},{8,9},{9,10... | collective-permute-start | bytes 393224 | tf_op jit(solution)/shard_map/ppermute | solution.py:30
  39.2 20.1 %collective-permute-start.15 = (bf16[64,4096]{1,0:T(8,128)(2,1)S(1)}, bf16[64,4096]{1,0:T(8,128)(2,1)S(1)}, u32[]{:S(2)}, u32[]{:S(2)}) collective-permute-start(bf16[64,4096]{1,0:T(8,128)(2,1)S(1)} %reshape.66.refs_5_), channel_id=1, source_target_pairs={{7,0},{0,1},{1,2},{2,3},{3,4},{4,5},{5,6},{6,7},{15,8},{8,9},{9,10... | collective-permute-start | bytes 1572872 | tf_op jit(solution)/shard_map/ppermute | solution.py:30
  39.3 20.0 %collective-permute-start.11 = (bf16[64,4096]{1,0:T(8,128)(2,1)S(1)}, bf16[64,4096]{1,0:T(8,128)(2,1)S(1)}, u32[]{:S(2)}, u32[]{:S(2)}) collective-permute-start(bf16[64,4096]{1,0:T(8,128)(2,1)S(1)} %reshape.66.refs_5_), channel_id=1, source_target_pairs={{1,0},{2,1},{3,2},{4,3},{5,4},{6,5},{7,6},{0,7},{9,8},{10,9},{11,1... | collective-permute-start | bytes 1572872 | tf_op jit(solution)/shard_map/ppermute | solution.py:30
  41.9 12.0 %collective-permute-start.3 = (bf16[16,4096]{1,0:T(8,128)(2,1)}, bf16[16,4096]{1,0:T(8,128)(2,1)S(1)}, u32[]{:S(2)}, u32[]{:S(2)}) collective-permute-start(bf16[16,4096]{1,0:T(8,128)(2,1)} %collective-permute-done.2), channel_id=1, source_target_pairs={{1,0},{2,1},{3,2},{4,3},{5,4},{6,5},{7,6},{0,7},{9,8},{10,9},{11,1... | collective-permute-start | bytes 393224 | tf_op jit(solution)/shard_map/ppermute | solution.py:30
  56.6 22.9 %collective-permute-start.9 = (bf16[128,4096]{1,0:T(8,128)(2,1)}, bf16[128,4096]{1,0:T(8,128)(2,1)S(1)}, u32[]{:S(2)}, u32[]{:S(2)}) collective-permute-start(bf16[128,4096]{1,0:T(8,128)(2,1)} %constant_dynamic-update-slice_fusion.refs_0_), channel_id=1, source_target_pairs={{24,0},{0,8},{8,16},{16,24},{25,1},{1,9},{9,17},{17,25},{26,2},{2,... | collective-permute-start | bytes 3145736 | tf_op jit(solution)/shard_map/ppermute | solution.py:30
  57.8 21.8 %collective-permute-start.7 = (bf16[128,4096]{1,0:T(8,128)(2,1)}, bf16[128,4096]{1,0:T(8,128)(2,1)S(1)}, u32[]{:S(2)}, u32[]{:S(2)}) collective-permute-start(bf16[128,4096]{1,0:T(8,128)(2,1)} %constant_dynamic-update-slice_fusion.refs_0_), channel_id=1, source_target_pairs={{8,0},{16,8},{24,16},{0,24},{9,1},{17,9},{25,17},{1,25},{10,2},{18... | collective-permute-start | bytes 3145736 | tf_op jit(solution)/shard_map/ppermute | solution.py:30
  59.3 11.8 %collective-permute-start.16 = (bf16[64,4096]{1,0:T(8,128)(2,1)S(1)}, bf16[64,4096]{1,0:T(8,128)(2,1)S(1)}, u32[]{:S(2)}, u32[]{:S(2)}) collective-permute-start(bf16[64,4096]{1,0:T(8,128)(2,1)S(1)} %collective-permute-done.15.refs_13_), channel_id=1, source_target_pairs={{7,0},{0,1},{1,2},{2,3},{3,4},{4,5},{5,6},{6,7},{15,8},{8,9},{9,10... | collective-permute-start | bytes 1572872 | tf_op jit(solution)/shard_map/ppermute | solution.py:30
  59.3 11.8 %collective-permute-start.12 = (bf16[64,4096]{1,0:T(8,128)(2,1)S(1)}, bf16[64,4096]{1,0:T(8,128)(2,1)S(1)}, u32[]{:S(2)}, u32[]{:S(2)}) collective-permute-start(bf16[64,4096]{1,0:T(8,128)(2,1)S(1)} %collective-permute-done.11.refs_6_), channel_id=1, source_target_pairs={{1,0},{2,1},{3,2},{4,3},{5,4},{6,5},{7,6},{0,7},{9,8},{10,9},{11,1... | collective-permute-start | bytes 1572872 | tf_op jit(solution)/shard_map/ppermute | solution.py:30
  100.6 13.4 %collective-permute-start.19 = (bf16[128,2688]{1,0:T(8,128)(2,1)S(1)}, bf16[128,2688]{1,0:T(8,128)(2,1)S(1)}, u32[]{:S(2)}, u32[]{:S(2)}) collective-permute-start(bf16[128,2688]{1,0:T(8,128)(2,1)S(1)} %get-tuple-element.35), channel_id=1, source_target_pairs={{24,0},{0,8},{8,16},{16,24},{25,1},{1,9},{9,17},{17,25},{26,2},{2,... | collective-permute-start | bytes 2064392 | tf_op jit(solution)/shard_map/ppermute | solution.py:30
  101.0 28.4 %collective-permute-start.20 = (bf16[128,2688]{1,0:T(8,128)(2,1)S(1)}, bf16[128,2688]{1,0:T(8,128)(2,1)S(1)}, u32[]{:S(2)}, u32[]{:S(2)}) collective-permute-start(bf16[128,2688]{1,0:T(8,128)(2,1)S(1)} %get-tuple-element.36), channel_id=1, source_target_pairs={{16,0},{24,8},{0,16},{8,24},{17,1},{25,9},{1,17},{9,25},{18,2},{26... | collective-permute-start | bytes 2064392 | tf_op jit(solution)/shard_map/ppermute | solution.py:30
  104.3 29.6 %collective-permute-start.21 = (bf16[128,2688]{1,0:T(8,128)(2,1)S(1)}, bf16[128,2688]{1,0:T(8,128)(2,1)S(1)}, u32[]{:S(2)}, u32[]{:S(2)}) collective-permute-start(bf16[128,2688]{1,0:T(8,128)(2,1)S(1)} %get-tuple-element.37), channel_id=1, source_target_pairs={{8,0},{16,8},{24,16},{0,24},{9,1},{17,9},{25,17},{1,25},{10,2},{18... | collective-permute-start | bytes 2064392 | tf_op jit(solution)/shard_map/ppermute | solution.py:30
  105.0 31.5 %collective-permute-start.29 = (bf16[64,1536]{1,0:T(8,128)(2,1)S(1)}, bf16[64,1536]{1,0:T(8,128)(2,1)S(1)}, u32[]{:S(2)}, u32[]{:S(2)}) collective-permute-start(bf16[64,1536]{1,0:T(8,128)(2,1)S(1)} %get-tuple-element.47), channel_id=1, source_target_pairs={{4,0},{5,1},{6,2},{7,3},{0,4},{1,5},{2,6},{3,7},{12,8},{13,9},{14,... | collective-permute-start | bytes 589832 | tf_op jit(solution)/shard_map/ppermute | solution.py:30
  109.0 29.7 %collective-permute-start.30 = (bf16[64,1536]{1,0:T(8,128)(2,1)S(1)}, bf16[64,1536]{1,0:T(8,128)(2,1)S(1)}, u32[]{:S(2)}, u32[]{:S(2)}) collective-permute-start(bf16[64,1536]{1,0:T(8,128)(2,1)S(1)} %get-tuple-element.48), channel_id=1, source_target_pairs={{5,0},{6,1},{7,2},{0,3},{1,4},{2,5},{3,6},{4,7},{13,8},{14,9},{15,... | collective-permute-start | bytes 589832 | tf_op jit(solution)/shard_map/ppermute | solution.py:30
  113.9 25.3 %collective-permute-start.31 = (bf16[64,1536]{1,0:T(8,128)(2,1)S(1)}, bf16[64,1536]{1,0:T(8,128)(2,1)S(1)}, u32[]{:S(2)}, u32[]{:S(2)}) collective-permute-start(bf16[64,1536]{1,0:T(8,128)(2,1)S(1)} %get-tuple-element.49), channel_id=1, source_target_pairs={{3,0},{4,1},{5,2},{6,3},{7,4},{0,5},{1,6},{2,7},{11,8},{12,9},{13,... | collective-permute-start | bytes 589832 | tf_op jit(solution)/shard_map/ppermute | solution.py:30
  129.4 13.7 %collective-permute-start.32 = (bf16[64,1536]{1,0:T(8,128)(2,1)S(1)}, bf16[64,1536]{1,0:T(8,128)(2,1)S(1)}, u32[]{:S(2)}, u32[]{:S(2)}) collective-permute-start(bf16[64,1536]{1,0:T(8,128)(2,1)S(1)} %get-tuple-element.50), channel_id=1, source_target_pairs={{6,0},{7,1},{0,2},{1,3},{2,4},{3,5},{4,6},{5,7},{14,8},{15,9},{8,1... | collective-permute-start | bytes 589832 | tf_op jit(solution)/shard_map/ppermute | solution.py:30
  133.9 11.6 %collective-permute-start.33 = (bf16[64,1536]{1,0:T(8,128)(2,1)S(1)}, bf16[64,1536]{1,0:T(8,128)(2,1)S(1)}, u32[]{:S(2)}, u32[]{:S(2)}) collective-permute-start(bf16[64,1536]{1,0:T(8,128)(2,1)S(1)} %get-tuple-element.51), channel_id=1, source_target_pairs={{2,0},{3,1},{4,2},{5,3},{6,4},{7,5},{0,6},{1,7},{10,8},{11,9},{12,... | collective-permute-start | bytes 589832 | tf_op jit(solution)/shard_map/ppermute | solution.py:30
  139.2 31.0 %collective-permute-start.22 = (bf16[16,2688]{1,0:T(8,128)(2,1)S(1)}, bf16[16,2688]{1,0:T(8,128)(2,1)S(1)}, u32[]{:S(2)}, u32[]{:S(2)}) collective-permute-start(bf16[16,2688]{1,0:T(8,128)(2,1)S(1)} %get-tuple-element.39), channel_id=1, source_target_pairs={{4,0},{5,1},{6,2},{7,3},{0,4},{1,5},{2,6},{3,7},{12,8},{13,9},{14,... | collective-permute-start | bytes 258056 | tf_op jit(solution)/shard_map/ppermute | solution.py:30
  143.1 27.1 %collective-permute-start.23 = (bf16[16,2688]{1,0:T(8,128)(2,1)S(1)}, bf16[16,2688]{1,0:T(8,128)(2,1)S(1)}, u32[]{:S(2)}, u32[]{:S(2)}) collective-permute-start(bf16[16,2688]{1,0:T(8,128)(2,1)S(1)} %get-tuple-element.40), channel_id=1, source_target_pairs={{5,0},{6,1},{7,2},{0,3},{1,4},{2,5},{3,6},{4,7},{13,8},{14,9},{15,... | collective-permute-start | bytes 258056 | tf_op jit(solution)/shard_map/ppermute | solution.py:30
  150.6 26.9 %all-to-all-start.3 = ((bf16[32,2,1536]{2,1,0:T(2,128)(2,1)}), bf16[32,2,1536]{2,1,0:T(2,128)(2,1)S(1)}, u32[]{:S(2)}, u32[]{:S(2)}) async-start(bf16[32,2,1536]{2,1,0:T(2,128)(2,1)} %bitcast.5), calls=%async_computation.3 | async-start | bytes 393216 | tf_op jit(solution)/shard_map/all_to_all | solution.py:337
  161.2 16.3 %collective-permute-start.24 = (bf16[16,2688]{1,0:T(8,128)(2,1)S(1)}, bf16[16,2688]{1,0:T(8,128)(2,1)S(1)}, u32[]{:S(2)}, u32[]{:S(2)}) collective-permute-start(bf16[16,2688]{1,0:T(8,128)(2,1)S(1)} %get-tuple-element.41), channel_id=1, source_target_pairs={{3,0},{4,1},{5,2},{6,3},{7,4},{0,5},{1,6},{2,7},{11,8},{12,9},{13,... | collective-permute-start | bytes 258056 | tf_op jit(solution)/shard_map/ppermute | solution.py:30
  164.2 13.4 %collective-permute-start.25 = (bf16[16,2688]{1,0:T(8,128)(2,1)S(1)}, bf16[16,2688]{1,0:T(8,128)(2,1)S(1)}, u32[]{:S(2)}, u32[]{:S(2)}) collective-permute-start(bf16[16,2688]{1,0:T(8,128)(2,1)S(1)} %get-tuple-element.42), channel_id=1, source_target_pairs={{6,0},{7,1},{0,2},{1,3},{2,4},{3,5},{4,6},{5,7},{14,8},{15,9},{8,1... | collective-permute-start | bytes 258056 | tf_op jit(solution)/shard_map/ppermute | solution.py:30
  164.7 12.9 %collective-permute-start.26 = (bf16[16,2688]{1,0:T(8,128)(2,1)S(1)}, bf16[16,2688]{1,0:T(8,128)(2,1)S(1)}, u32[]{:S(2)}, u32[]{:S(2)}) collective-permute-start(bf16[16,2688]{1,0:T(8,128)(2,1)S(1)} %get-tuple-element.43), channel_id=1, source_target_pairs={{2,0},{3,1},{4,2},{5,3},{6,4},{7,5},{0,6},{1,7},{10,8},{11,9},{12,... | collective-permute-start | bytes 258056 | tf_op jit(solution)/shard_map/ppermute | solution.py:30
  (21 other events, 356.9 us)
